TPU v7x, 256 devices: a whole 4x4x8 slice. The times are simulated.
256 devices in a mesh: loader: 64 (over z, x, core), split: 4 (over y).
Axes of the slice: x: 4, y: 4, z: 8, core: 2. Of those that a mesh axis runs over, the one named last changes fastest.
Arguments:
- embeddings: bfloat16 [131072, 768], P(('loader', 'split')), may hold values from -6 to 6
- cluster_ids: int32 [131072, 1], P(('loader', 'split')), may hold values from 0 to 255; in each aligned block of 512 rows (0 to 511, 512 to 1023, ...) at most 4 rows name the same one
- ranks: int32 [131072], P(('loader', 'split')), may hold values from 0 to 131071, each once
Outputs:
- nearest: float32 [131072], P(('loader', 'split'))
Inputs may be any that keep to these rules, and one draw needn't show every extreme that they name: `cluster_ids`: among the 512 rows of one device no cluster appears more than 4 times. All ranks differ.
All inputs are finite; a program needn't handle non-finite values.
Results may differ from a plain program's by a relative error of at most 0.0014.
Values may be sent and summed in bfloat16 or wider, within the bound.
No kernel may reach another device: no remote copies, remote signals or barrier semaphores. Data moves between devices by JAX's collectives and lax.ppermute only.
A program may use at most 64 MiB of HBM per device.

v0:
```python
import jax
import jax.numpy as jnp
from jax import lax
from jax.sharding import PartitionSpec as P

CLUSTERS = 256
CAP = 4


epsilon = 1e-06


def in_blocks(x, dim, size):
    dims = x.shape
    parts = x.reshape(*dims[:dim], size, dims[dim] // size, *dims[dim + 1 :])
    return jnp.moveaxis(parts, dim, 0)


def laid_out(parts, dim):
    dims = list(parts.shape[1:])
    dims[dim] *= parts.shape[0]
    return jnp.moveaxis(parts, 0, dim).reshape(dims)


def joined_exchange(x, axis, axes, splits, concats):
    sizes = [lax.axis_size(a) for a in axes]
    parts = in_blocks(x, splits[0], sizes[0])
    parts = jnp.moveaxis(in_blocks(parts, splits[1] + 1, sizes[1]), 0, 1)
    inside = parts.shape[2:]
    parts = parts.reshape(-1, *inside)
    parts = lax.all_to_all(parts, axis, split_axis=0, concat_axis=0, tiled=True)
    parts = laid_out(parts.reshape(*sizes, *inside), concats[0] + 1)
    return laid_out(parts, concats[1])


def tile_scores(queries, remote):
    return jnp.einsum("kqd,kmd->kqm", queries, remote, preferred_element_type=jnp.float32)


def row_maxima(scores, query_rank, member_rank):
    allowed = (member_rank[:, None, :] >= 0) & (member_rank[:, None, :] < query_rank[:, :, None])
    return jnp.max(jnp.where(allowed, scores, jnp.float32(-1.0)), axis=2)


def shards(embeddings, cluster_ids, ranks):
    loader_count = lax.axis_size("loader")
    split_count = lax.axis_size("split")
    rows_here = embeddings.shape[0]
    width = embeddings.shape[1]
    values = embeddings.astype(jnp.float32)
    unit = (values * lax.rsqrt(jnp.sum(values * values, axis=1, keepdims=True) + epsilon)).astype(
        jnp.bfloat16
    )
    cluster = cluster_ids[:, 0]
    row_index = jnp.arange(rows_here, dtype=jnp.int32)
    same_cluster = cluster[:, None] == cluster[None, :]
    earlier = row_index[None, :] < row_index[:, None]
    position = jnp.sum((same_cluster & earlier).astype(jnp.int32), axis=1)
    slot_count = CLUSTERS * CAP
    device_count = loader_count * split_count
    owner_flat = cluster % device_count
    cluster_slot = cluster // device_count
    owned = CLUSTERS // device_count
    target = (
        (cluster_slot * loader_count + owner_flat // split_count) * split_count
        + owner_flat % split_count
    ) * CAP + position
    send_rows = (
        jnp.zeros((slot_count, width), jnp.bfloat16)
        .at[target]
        .set(unit)
        .reshape(owned, loader_count, split_count, CAP, width)
    )
    send_rank = (
        jnp.full((slot_count,), -1, jnp.int32)
        .at[target]
        .set(ranks)
        .reshape(owned, loader_count, split_count, CAP)
    )
    arrived_rows, arrived_rank = (
        joined_exchange(send_rows, ("loader", "split"), ("loader", "split"), (1, 2), (1, 2)),
        joined_exchange(send_rank, ("loader", "split"), ("loader", "split"), (1, 2), (1, 2)),
    )
    members = arrived_rows.reshape(owned, -1, width)
    member_rank = arrived_rank.reshape(owned, -1)
    best = row_maxima(tile_scores(members, members), member_rank, member_rank)
    best = best.reshape(owned, loader_count, split_count, CAP)
    returned = joined_exchange(best, ("loader", "split"), ("loader", "split"), (1, 2), (1, 2))
    return returned.reshape(-1)[target]


def solution(mesh):
    return jax.shard_map(
        shards,
        mesh=mesh,
        in_specs=(
            P(("loader", "split"), None),
            P(("loader", "split"), None),
            P(("loader", "split")),
        ),
        out_specs=P(("loader", "split")),
        check_vma=False,
    )
```

profile of v0, /device:TPU:1, one launch (start us, length us, event | category | flops | bytes accessed | tf_op | source)
XLA Modules:
  0.0 108.8 jit_solution(2060933318394215782)
XLA Ops:
  0.0 0.0 copy-start
  0.0 1.0 convert_reduce_fusion
  1.0 0.7 compare_select_fusion
  1.7 2.6 %scatter_custom_fusion = s32[1024]{0:T(1024)S(1)} fusion(s32[512]{0:T(512)S(1)} %bitcast.39, s32[512]{0:T(512)} %param.5, s32[]{:T(128)} %constant.51.clone.1), kind=kCustom, calls=%fused_computation.29 | custom fusion | bytes 4608 | tf_op jit(solution)/shard_map/scatter | solution.py:77
  4.4 0.8 reshape_transpose_transpose_reshape_transpose_reshape_reshape.9
  5.1 15.6 %all-to-all-start = ((s32[256,1,1,1,4]{4,3,2,1,0:T(1,128)}), s32[256,1,1,1,4]{4,3,2,1,0:T(1,128)S(1)}, u32[]{:S(2)}, u32[]{:S(2)}) async-start(s32[256,1,1,1,4]{4,3,2,1,0:T(1,128)} %bitcast.3), calls=%async_computation | async-start | bytes 262144 | tf_op jit(solution)/shard_map/all_to_all | solution.py:31
  20.8 1.4 %fusion = f32[512]{0:T(512)S(1)} fusion(bf16[512,768]{1,0:T(8,128)(2,1)} %param.3), kind=kLoop, calls=%fused_computation.6 | loop fusion | flops 1179136 | bytes 788480 | tf_op jit(solution)/shard_map/reduce_sum | solution.py:51
  22.2 0.0 copy-done
  22.2 3.1 %scatter_custom_fusion.1 = bf16[1024,768]{1,0:T(8,128)(2,1)S(1)} fusion(s32[512]{0:T(512)S(1)} %bitcast.40, bf16[512,768]{1,0:T(8,128)(2,1)S(1)} %copy-done, f32[512]{0:T(512)S(1)} %add_rsqrt_fusion, bf16[]{:T(256)} %constant.62.clone.1), kind=kCustom, calls=%fused_computation.11 | custom fusion | flops 1179648 | bytes 2361346 | tf_op jit(solution)/shard_map/scatter | solution.py:71
  25.3 1.4 %reshape_transpose_transpose_reshape_transpose_reshape_reshape.10 = bf16[256,1,1,1,4,768]{5,4,0,3,2,1:T(4,128)(2,1)} reshape(bf16[1024,768]{1,0:T(8,128)(2,1)S(1)} %scatter_custom_fusion.1) | data formatting | bytes 3145728 | tf_op jit(solution)/shard_map/reshape;transpose;transpose;reshape;transpose;reshape;reshape | solution.py:30
  26.6 6.9 %all-to-all-done = s32[256,1,1,1,4]{4,3,2,1,0:T(1,128)S(1)} async-done(((s32[256,1,1,1,4]{4,3,2,1,0:T(1,128)}), s32[256,1,1,1,4]{4,3,2,1,0:T(1,128)S(1)}, u32[]{:S(2)}, u32[]{:S(2)}) %all-to-all-start) | async-done | bytes 4128 | tf_op jit(solution)/shard_map/all_to_all | solution.py:31
  33.5 6.8 %all-to-all-start.1 = ((bf16[256,1,1,1,4,768]{5,4,3,2,1,0:T(4,128)(2,1)}), bf16[256,1,1,1,4,768]{5,4,3,2,1,0:T(4,128)(2,1)S(1)}, u32[]{:S(2)}, u32[]{:S(2)}) async-start(bf16[256,1,1,1,4,768]{5,4,3,2,1,0:T(4,128)(2,1)} %bitcast.8), calls=%async_computation.1 | async-start | bytes 3145728 | tf_op jit(solution)/shard_map/all_to_all | solution.py:31
  40.4 0.2 broadcast_in_dim_reshape_reshape.2
  40.5 41.9 %all-to-all-done.1 = bf16[256,1,1,1,4,768]{5,4,3,2,1,0:T(4,128)(2,1)S(1)} async-done(((bf16[256,1,1,1,4,768]{5,4,3,2,1,0:T(4,128)(2,1)}), bf16[256,1,1,1,4,768]{5,4,3,2,1,0:T(4,128)(2,1)S(1)}, u32[]{:S(2)}, u32[]{:S(2)}) %all-to-all-start.1) | async-done | bytes 1572896 | tf_op jit(solution)/shard_map/all_to_all | solution.py:31
  82.4 0.4 reshape.57
  82.8 2.3 %select_reduce_fusion = f32[1024]{0:T(1024)S(1)} fusion(s32[1024]{0:T(1024)S(1)} %broadcast_in_dim_reshape_reshape.2, pred[1024]{0:T(1024)(128)(4,1)S(1)} %broadcast_compare_fusion, bf16[1024,768]{1,0:T(8,128)(2,1)S(1)} %reshape.57), kind=kOutput, calls=%fused_computation.3 | convolution fusion | flops 1614806016 | bytes 1582080 | tf_op jit(solution)/shard_map/kqd,kmd->kqm/dot_general | solution.py:37
  85.0 0.8 reshape_transpose_transpose_reshape_transpose_reshape_reshape.11
  85.8 6.7 %all-to-all-start.2 = ((f32[256,1,1,1,4]{4,3,2,1,0:T(1,128)}), f32[256,1,1,1,4]{4,3,2,1,0:T(1,128)S(1)}, u32[]{:S(2)}, u32[]{:S(2)}) async-start(f32[256,1,1,1,4]{4,3,2,1,0:T(1,128)} %bitcast.13), calls=%async_computation.2 | async-start | bytes 262144 | tf_op jit(solution)/shard_map/all_to_all | solution.py:31
  92.5 12.7 %all-to-all-done.2 = f32[256,1,1,1,4]{4,3,2,1,0:T(1,128)S(1)} async-done(((f32[256,1,1,1,4]{4,3,2,1,0:T(1,128)}), f32[256,1,1,1,4]{4,3,2,1,0:T(1,128)S(1)}, u32[]{:S(2)}, u32[]{:S(2)}) %all-to-all-start.2) | async-done | bytes 4128 | tf_op jit(solution)/shard_map/all_to_all | solution.py:31
  105.2 0.2 reshape_reshape.4
  105.4 3.4 %gather_fusion = f32[512]{0:T(512)} fusion(f32[1024]{0:T(1024)S(1)} %reshape_reshape.4, s32[1024]{0:T(1024)S(1)} %pad_clamp_fusion), kind=kCustom, calls=%fused_computation | custom fusion | bytes 6144 | tf_op jit(solution)/shard_map/gather | solution.py:89
  (3 shorter events, 0.0 us)
Async XLA Ops:
  0.0 22.2 %copy-start = (bf16[512,768]{1,0:T(8,128)(2,1)S(1)}, bf16[512,768]{1,0:T(8,128)(2,1)}, u32[]{:S(2)}) copy-start(bf16[512,768]{1,0:T(8,128)(2,1)} %param.3) | copy-start | bytes 2359300
  5.1 28.4 %all-to-all-start = ((s32[256,1,1,1,4]{4,3,2,1,0:T(1,128)}), s32[256,1,1,1,4]{4,3,2,1,0:T(1,128)S(1)}, u32[]{:S(2)}, u32[]{:S(2)}) async-start(s32[256,1,1,1,4]{4,3,2,1,0:T(1,128)} %bitcast.3), calls=%async_computation | async-start | bytes 262144 | tf_op jit(solution)/shard_map/all_to_all | solution.py:31
  33.5 48.9 %all-to-all-start.1 = ((bf16[256,1,1,1,4,768]{5,4,3,2,1,0:T(4,128)(2,1)}), bf16[256,1,1,1,4,768]{5,4,3,2,1,0:T(4,128)(2,1)S(1)}, u32[]{:S(2)}, u32[]{:S(2)}) async-start(bf16[256,1,1,1,4,768]{5,4,3,2,1,0:T(4,128)(2,1)} %bitcast.8), calls=%async_computation.1 | async-start | bytes 3145728 | tf_op jit(solution)/shard_map/all_to_all | solution.py:31
  85.8 19.4 %all-to-all-start.2 = ((f32[256,1,1,1,4]{4,3,2,1,0:T(1,128)}), f32[256,1,1,1,4]{4,3,2,1,0:T(1,128)S(1)}, u32[]{:S(2)}, u32[]{:S(2)}) async-start(f32[256,1,1,1,4]{4,3,2,1,0:T(1,128)} %bitcast.13), calls=%async_computation.2 | async-start | bytes 262144 | tf_op jit(solution)/shard_map/all_to_all | solution.py:31
where the time goes:
time: 109 us
  waiting for transfers between devices  61.5 us (56%)
  starting transfers between devices  29.1 us (27%)
  local copies, waits for them, and re-layouts  9.62 us (9%)
  other arithmetic  6.23 us (6%)
  matrix products  2.27 us (2%)
    all_to_all x3, waiting for transfers between devices, joined_exchange(): parts = lax.all_to_all(parts, axis, split_axis=0, concat_axis=0, tiled=True)  61.5 us
    all_to_all x3, starting transfers between devices, joined_exchange(): parts = lax.all_to_all(parts, axis, split_axis=0, concat_axis=0, tiled=True)  29.1 us
    gather x1, local copies, waits for them, and re-layouts, shards(): return returned.reshape(-1)[target]  3.42 us
    scatter x1, other arithmetic, shards(): send_rows = jnp.zeros((slot_count, width), jnp.bfloat16).at[target].set(u...  3.1 us
    another operation x3, local copies, waits for them, and re-layouts, joined_exchange(): parts = parts.reshape(-1, *inside)  2.91 us
    scatter x1, local copies, waits for them, and re-layouts, shards(): send_rank = jnp.full((slot_count,), -1, jnp.int32).at[target].set(ranks)....  2.6 us
    dot_general x1, matrix products, tile_scores(): jnp.einsum('kqd,kmd->kqm', queries, remote, preferred_element_type=jnp.fl...  2.27 us
  transfers between devices with their start and end apart: 3, of which 3 were waited for; matrix products, arithmetic and copies ran while one was open for 6% of the time, Pallas kernels for 0%

commit v1 on v0

v1 whole, which is shorter than its diff:
```python
import jax
import jax.numpy as jnp
from jax import lax
from jax.experimental import pallas as pl
from jax.experimental.pallas import tpu as pltpu
from jax.sharding import PartitionSpec as P

CLUSTERS = 256
CAP = 4
LANES = 128
BLOCKS = 4
DIGIT = 64
AXES = ("loader", "split")
VMEM = pl.BlockSpec(memory_space=pltpu.VMEM)

epsilon = 1e-06


def iota(dims, dim):
    return lax.broadcasted_iota(jnp.int32, dims, dim)


def flag(mask):
    return mask.astype(jnp.float32).astype(jnp.bfloat16)


def dot(a, b, contract_b=0):
    return lax.dot_general(
        a, b, (((1,), (contract_b,)), ((), ())), preferred_element_type=jnp.float32
    )


def pack(ids_ref, rank_ref, rows_ref, out_ref, target_ref, held, unit_ref, digit_ref, slot_ref, sem):
    rows, width = held.shape
    step = pl.program_id(0)

    @pl.when(step == 0)
    def prepare():
        load = pltpu.make_async_copy(rows_ref, held, sem)
        load.start()
        cluster = ids_ref[...]
        member = iota((CLUSTERS, rows), 0) == cluster
        before = iota((rows, rows), 0) < iota((rows, rows), 1)
        count = dot(flag(member), flag(before))
        position = jnp.sum(jnp.where(member, count, 0.0), axis=0, keepdims=True).astype(jnp.int32)
        target = cluster * CAP + position
        target_ref[...] = target
        slot_ref[...] = target
        rank = rank_ref[...] + 1
        which = iota((LANES, rows), 0)
        high, middle, low = rank // (DIGIT * DIGIT), rank // DIGIT % DIGIT, rank % DIGIT
        which = jnp.where(which >= 3, which - 3, which)
        digits = jnp.where(which == 0, high, jnp.where(which == 1, middle, jnp.where(which == 2, low, 0)))
        digit_ref[...] = digits.astype(jnp.float32).astype(jnp.bfloat16)
        load.wait()
        values = held[...].astype(jnp.float32)
        scale = lax.rsqrt(jnp.sum(values * values, axis=1, keepdims=True) + epsilon)
        unit_ref[...] = (values * scale).astype(jnp.bfloat16)

    owners = CLUSTERS // BLOCKS
    pairs = owners * 2
    target = slot_ref[...]
    local = iota((pairs, rows), 0)
    wanted = (local // 2 + step * owners) * CAP + local % 2
    pick = jnp.concatenate([flag(wanted == target), flag(wanted + 2 == target)], axis=0)
    packed = dot(pick, unit_ref[...]).astype(jnp.bfloat16)
    out_ref[:, :, :width] = packed[:pairs].reshape(owners, 2, width)
    out_ref[:, :, width : 2 * width] = packed[pairs:].reshape(owners, 2, width)
    digits = dot(pick, digit_ref[...], 1)
    digits = jnp.where(iota((pairs, LANES), 1) < 3, digits[:pairs], digits[pairs:])
    out_ref[:, :, 2 * width :] = digits.astype(jnp.bfloat16).reshape(owners, 2, LANES)


def score(rows_ref, out_ref, keys_ref, best_ref):
    sources, _, wide = rows_ref.shape
    slots, width = keys_ref.shape
    half = slots // 2
    block = 256
    keys_ref[:half, :] = rows_ref[:, :, :width].reshape(half, width)
    keys_ref[half:, :] = rows_ref[:, :, width : 2 * width].reshape(half, width)
    digits = rows_ref[:, :, 2 * width :].reshape(half, LANES)
    def weights(dims, dim, other, size):
        place = iota(dims, dim) - 3 * (iota(dims, other) // size)
        value = jnp.where(place == 0, DIGIT * DIGIT, jnp.where(place == 1, DIGIT, jnp.where(place == 2, 1, 0)))
        return value.astype(jnp.float32).astype(jnp.bfloat16)
    column = dot(digits, weights((LANES, 2 * LANES), 0, 1, LANES))
    row = dot(weights((8, LANES), 1, 0, 1), digits, 1)
    row = jnp.where(row == 0.0, 1e9, row)
    keys = keys_ref[...]
    for q in range(slots // block):
        scores = dot(keys_ref[q * block : (q + 1) * block, :], keys, 1)
        side, start = divmod(q * block, half)
        query_rank = column[start : start + block, side * LANES : (side + 1) * LANES]
        best = jnp.full((block, LANES), -1.0, jnp.float32)
        for k in range(slots // LANES):
            part = k * LANES
            key_rank = row[part // half : part // half + 1, part % half : part % half + LANES]
            allowed = key_rank < query_rank
            best = jnp.maximum(best, jnp.where(allowed, scores[:, part : part + LANES], -1.0))
        best_ref[q * block : (q + 1) * block, :] = jnp.broadcast_to(
            jnp.max(best, axis=1, keepdims=True), (block, LANES)
        )
    lane = iota((sources, LANES), 1)
    out = best_ref[pl.ds(0, sources, stride=2), :]
    for p in range(1, CAP):
        start = p // 2 * half + p % 2
        out = jnp.where(lane == p, best_ref[pl.ds(start, sources, stride=2), :], out)
    out_ref[...] = out


def unpack(back_ref, target_ref, out_ref):
    rows = target_ref.shape[1]
    back = back_ref[...]
    target = target_ref[...]
    position = target % CAP
    value = jnp.broadcast_to(back[:, 0:1], (CLUSTERS, rows))
    for p in range(1, CAP):
        value = jnp.where(position == p, jnp.broadcast_to(back[:, p : p + 1], (CLUSTERS, rows)), value)
    member = iota((CLUSTERS, rows), 0) == target // CAP
    out_ref[...] = jnp.sum(jnp.where(member, value, 0.0), axis=0, keepdims=True)


def on_chip(x):
    return pltpu.with_memory_space_constraint(x, pltpu.VMEM)


def exchange(x):
    return lax.all_to_all(x, AXES, 0, 0, tiled=True)


def shards(embeddings, cluster_ids, ranks):
    rows, width = embeddings.shape
    slots = CLUSTERS * CAP
    wide = 2 * width + LANES
    f32, i32, bf16 = jnp.float32, jnp.int32, jnp.bfloat16
    shape = jax.ShapeDtypeStruct
    whole = lambda dims: pl.BlockSpec(dims, lambda i: (0,) * len(dims))
    packed, target = pl.pallas_call(
        pack,
        grid=(BLOCKS,),
        out_shape=(shape((CLUSTERS, 2, wide), bf16), shape((1, rows), i32)),
        in_specs=[whole((1, rows)), whole((1, rows)), pl.BlockSpec(memory_space=pl.ANY)],
        out_specs=(
            pl.BlockSpec((CLUSTERS // BLOCKS, 2, wide), lambda i: (i, 0, 0)),
            whole((1, rows)),
        ),
        scratch_shapes=[
            pltpu.VMEM((rows, width), bf16),
            pltpu.VMEM((rows, width), bf16),
            pltpu.VMEM((LANES, rows), bf16),
            pltpu.VMEM((1, rows), i32),
            pltpu.SemaphoreType.DMA,
        ],
        name="pack",
    )(cluster_ids.reshape(1, rows), ranks.reshape(1, rows), embeddings)
    arrived = exchange(packed)
    best = pl.pallas_call(
        score,
        out_shape=pltpu.VMEM((CLUSTERS, LANES), f32),
        in_specs=[VMEM],
        out_specs=VMEM,
        scratch_shapes=[pltpu.VMEM((slots, width), bf16), pltpu.VMEM((slots, LANES), f32)],
        name="score",
    )(on_chip(arrived))
    back = exchange(best.reshape(CLUSTERS, 1, LANES)).reshape(CLUSTERS, LANES)
    out = pl.pallas_call(
        unpack, out_shape=shape((1, rows), f32), in_specs=[VMEM, VMEM], name="unpack"
    )(on_chip(back), target)
    return out.reshape(rows)


def solution(mesh):
    return jax.shard_map(
        shards,
        mesh=mesh,
        in_specs=(P(AXES, None), P(AXES, None), P(AXES)),
        out_specs=P(AXES),
        check_vma=False,
    )
```

time: 109 us -> 88.7 us (0.81)
  blocking collectives: 0 us -> 79.7 us
  waiting for transfers between devices: 61.5 us -> 0 us
  starting transfers between devices: 29.1 us -> 0 us
  local copies, waits for them, and re-layouts: 9.62 us -> 0 us
  Pallas kernels: 0 us -> 8.71 us
  other arithmetic: 6.23 us -> 0 us
  matrix products: 2.27 us -> 0 us
    all_to_all x0 -> x2, blocking collectives: none -> 79.7 us  [exchange(): return lax.all_to_all(x, AXES, 0, 0, tiled=True)]
    all_to_all x3 -> x0, waiting for transfers between devices: 61.5 us -> none  [joined_exchange(): parts = lax.all_to_all(parts, axis, split_axis=0, concat_axis=0, tiled=True)]
    all_to_all x3 -> x0, starting transfers between devices: 29.1 us -> none  [joined_exchange(): parts = lax.all_to_all(parts, axis, split_axis=0, concat_axis=0, tiled=True)]
    pallas_call x0 -> x3, Pallas kernels: none -> 8.71 us  [the longest x1 5.03 us: shards(): pl.pallas_call(pack, grid=(BLOCKS,), out_shape=(shape((CLUSTERS, 2, wide)...]
    another operation x6 -> x0, local copies, waits for them, and re-layouts: 3.59 us -> none  [the longest x3 2.91 us: joined_exchange(): parts = parts.reshape(-1, *inside)]
    gather x1 -> x0, local copies, waits for them, and re-layouts: 3.42 us -> none  [shards(): return returned.reshape(-1)[target]]
    scatter x1 -> x0, other arithmetic: 3.1 us -> none  [shards(): send_rows = jnp.zeros((slot_count, width), jnp.bfloat16).at[target].set(u...]
    scatter x1 -> x0, local copies, waits for them, and re-layouts: 2.6 us -> none  [shards(): send_rank = jnp.full((slot_count,), -1, jnp.int32).at[target].set(ranks)....]
  transfers between devices with their start and end apart: 3 -> 0, of which waited for: 3 -> 0; matrix products, arithmetic and copies ran while one was open for 6% -> 0% of each run, Pallas kernels for 0% -> 0%
where the time goes in v1:
time: 88.7 us; the launch traced here: 88.4 us
  blocking collectives  79.7 us (90%)
  Pallas kernels  8.71 us (10%)
    all_to_all x2, blocking collectives, exchange(): return lax.all_to_all(x, AXES, 0, 0, tiled=True)  79.7 us
    pallas_call x1, Pallas kernels, shards(): pl.pallas_call(pack, grid=(BLOCKS,), out_shape=(shape((CLUSTERS, 2, wide)...  5.03 us
    pallas_call x1, Pallas kernels, shards(): pl.pallas_call(score, out_shape=pltpu.VMEM((CLUSTERS, LANES), f32), in_sp...  2.14 us

profile of v1, /device:TPU:1, one launch (start us, length us, event | category | flops | bytes accessed | tf_op | source)
XLA Modules:
  0.0 88.4 jit_solution(16925466870438500379)
XLA Ops:
  0.0 5.0 %pack.1 = (bf16[256,2,1664]{2,1,0:T(2,128)(2,1)}, s32[1,512]{1,0:T(1,128)}) custom-call(s32[1,512]{1,0:T(1,128)} %bitcast.9, s32[1,512]{1,0:T(1,128)} %bitcast.10, bf16[512,768]{1,0:T(8,128)(2,1)} %rows_ref.1), custom_call_target="tpu_custom_call" | custom-call | tf_op jit(solution)/shard_map/pack/pallas_call | solution.py:138
  5.0 60.6 %all_to_all.10.rows_ref = bf16[256,2,1664]{2,1,0:T(2,128)(2,1)S(1)} all-to-all(bf16[256,2,1664]{2,1,0:T(2,128)(2,1)} %get-tuple-element.7), channel_id=1, replica_groups=mesh['loader'=64,'split'=4] {'loader','split'}, dimensions={0} | all-to-all | bytes 3407872 | tf_op jit(solution)/shard_map/all_to_all | solution.py:128
  65.7 2.1 %score.1 = f32[256,128]{1,0:T(8,128)S(1)} custom-call(bf16[256,2,1664]{2,1,0:T(2,128)(2,1)S(1)} %all_to_all.10.rows_ref), custom_call_target="tpu_custom_call" | custom-call | tf_op jit(solution)/shard_map/score/pallas_call | solution.py:157
  67.8 19.1 %all_to_all.11 = f32[256,1,128]{2,1,0:T(1,128)S(1)} all-to-all(f32[256,1,128]{2,1,0:T(1,128)S(1)} %bitcast.7), channel_id=1, replica_groups=mesh['loader'=64,'split'=4] {'loader','split'}, dimensions={0} | all-to-all | bytes 262144 | tf_op jit(solution)/shard_map/all_to_all | solution.py:128
  86.9 1.5 %unpack.1 = f32[1,512]{1,0:T(1,128)} custom-call(f32[256,128]{1,0:T(8,128)S(1)} %bitcast.8, s32[1,512]{1,0:T(1,128)} %get-tuple-element.8.target_ref), custom_call_target="tpu_custom_call" | custom-call | tf_op jit(solution)/shard_map/unpack/pallas_call | solution.py:166

commit v2 on v1

--- a/solution.py
+++ b/solution.py
@@ -9,6 +9,7 @@
 CAP = 4
 LANES = 128
 BLOCKS = 4
+CHUNKS = 4
 DIGIT = 64
 AXES = ("loader", "split")
 VMEM = pl.BlockSpec(memory_space=pltpu.VMEM)
@@ -30,45 +31,49 @@
     )
 
 
-def pack(ids_ref, rank_ref, rows_ref, out_ref, target_ref, held, unit_ref, digit_ref, slot_ref, sem):
+def pack(ids_hbm, rank_hbm, rows_hbm, out_ref, target_ref, ids_ref, rank_ref, held, unit_ref, digit_ref, sems):
     rows, width = held.shape
-    step = pl.program_id(0)
-
-    @pl.when(step == 0)
-    def prepare():
-        load = pltpu.make_async_copy(rows_ref, held, sem)
+    chunk = rows // CHUNKS
+    loads = [pltpu.make_async_copy(ids_hbm, ids_ref, sems.at[0]), pltpu.make_async_copy(rank_hbm, rank_ref, sems.at[1])]
+    for c in range(CHUNKS):
+        part = pl.ds(c * chunk, chunk)
+        loads.append(pltpu.make_async_copy(rows_hbm.at[part], held.at[part], sems.at[2 + c]))
+    for load in loads:
         load.start()
-        cluster = ids_ref[...]
-        member = iota((CLUSTERS, rows), 0) == cluster
-        before = iota((rows, rows), 0) < iota((rows, rows), 1)
-        count = dot(flag(member), flag(before))
-        position = jnp.sum(jnp.where(member, count, 0.0), axis=0, keepdims=True).astype(jnp.int32)
-        target = cluster * CAP + position
-        target_ref[...] = target
-        slot_ref[...] = target
-        rank = rank_ref[...] + 1
-        which = iota((LANES, rows), 0)
-        high, middle, low = rank // (DIGIT * DIGIT), rank // DIGIT % DIGIT, rank % DIGIT
-        which = jnp.where(which >= 3, which - 3, which)
-        digits = jnp.where(which == 0, high, jnp.where(which == 1, middle, jnp.where(which == 2, low, 0)))
-        digit_ref[...] = digits.astype(jnp.float32).astype(jnp.bfloat16)
-        load.wait()
-        values = held[...].astype(jnp.float32)
+    loads[0].wait()
+    loads[1].wait()
+    cluster = ids_ref[...]
+    member = iota((CLUSTERS, rows), 0) == cluster
+    before = iota((rows, rows), 0) < iota((rows, rows), 1)
+    count = dot(flag(member), flag(before))
+    position = jnp.sum(jnp.where(member, count, 0.0), axis=0, keepdims=True).astype(jnp.int32)
+    target = cluster * CAP + position
+    target_ref[...] = target
+    rank = rank_ref[...] + 1
+    which = iota((LANES, rows), 0)
+    which = jnp.where(which >= 3, which - 3, which)
+    high, middle, low = rank // (DIGIT * DIGIT), rank // DIGIT % DIGIT, rank % DIGIT
+    digits = jnp.where(which == 0, high, jnp.where(which == 1, middle, jnp.where(which == 2, low, 0)))
+    digit_ref[...] = digits.astype(jnp.float32).astype(jnp.bfloat16)
+    for c in range(CHUNKS):
+        loads[2 + c].wait()
+        values = held[c * chunk : (c + 1) * chunk, :].astype(jnp.float32)
         scale = lax.rsqrt(jnp.sum(values * values, axis=1, keepdims=True) + epsilon)
-        unit_ref[...] = (values * scale).astype(jnp.bfloat16)
-
+        unit_ref[c * chunk : (c + 1) * chunk, :] = (values * scale).astype(jnp.bfloat16)
     owners = CLUSTERS // BLOCKS
     pairs = owners * 2
-    target = slot_ref[...]
     local = iota((pairs, rows), 0)
-    wanted = (local // 2 + step * owners) * CAP + local % 2
-    pick = jnp.concatenate([flag(wanted == target), flag(wanted + 2 == target)], axis=0)
-    packed = dot(pick, unit_ref[...]).astype(jnp.bfloat16)
-    out_ref[:, :, :width] = packed[:pairs].reshape(owners, 2, width)
-    out_ref[:, :, width : 2 * width] = packed[pairs:].reshape(owners, 2, width)
-    digits = dot(pick, digit_ref[...], 1)
-    digits = jnp.where(iota((pairs, LANES), 1) < 3, digits[:pairs], digits[pairs:])
-    out_ref[:, :, 2 * width :] = digits.astype(jnp.bfloat16).reshape(owners, 2, LANES)
+    local = local // 2 * CAP + local % 2
+    for step in range(BLOCKS):
+        wanted = local + step * owners * CAP
+        pick = jnp.concatenate([flag(wanted == target), flag(wanted + 2 == target)], axis=0)
+        packed = dot(pick, unit_ref[...]).astype(jnp.bfloat16)
+        out = out_ref.at[step * owners : (step + 1) * owners]
+        out[:, :, :width] = packed[:pairs].reshape(owners, 2, width)
+        out[:, :, width : 2 * width] = packed[pairs:].reshape(owners, 2, width)
+        digits = dot(pick, digit_ref[...], 1)
+        digits = jnp.where(iota((pairs, LANES), 1) < 3, digits[:pairs], digits[pairs:])
+        out[:, :, 2 * width :] = digits.astype(jnp.bfloat16).reshape(owners, 2, LANES)
 
 
 def score(rows_ref, out_ref, keys_ref, best_ref):
@@ -134,22 +139,18 @@
     wide = 2 * width + LANES
     f32, i32, bf16 = jnp.float32, jnp.int32, jnp.bfloat16
     shape = jax.ShapeDtypeStruct
-    whole = lambda dims: pl.BlockSpec(dims, lambda i: (0,) * len(dims))
     packed, target = pl.pallas_call(
         pack,
-        grid=(BLOCKS,),
-        out_shape=(shape((CLUSTERS, 2, wide), bf16), shape((1, rows), i32)),
-        in_specs=[whole((1, rows)), whole((1, rows)), pl.BlockSpec(memory_space=pl.ANY)],
-        out_specs=(
-            pl.BlockSpec((CLUSTERS // BLOCKS, 2, wide), lambda i: (i, 0, 0)),
-            whole((1, rows)),
-        ),
+        out_shape=(pltpu.VMEM((CLUSTERS, 2, wide), bf16), pltpu.VMEM((1, rows), i32)),
+        in_specs=[pl.BlockSpec(memory_space=pl.ANY)] * 3,
+        out_specs=(VMEM, VMEM),
         scratch_shapes=[
+            pltpu.VMEM((1, rows), i32),
+            pltpu.VMEM((1, rows), i32),
             pltpu.VMEM((rows, width), bf16),
             pltpu.VMEM((rows, width), bf16),
             pltpu.VMEM((LANES, rows), bf16),
-            pltpu.VMEM((1, rows), i32),
-            pltpu.SemaphoreType.DMA,
+            pltpu.SemaphoreType.DMA((2 + CHUNKS,)),
         ],
         name="pack",
     )(cluster_ids.reshape(1, rows), ranks.reshape(1, rows), embeddings)
@@ -165,7 +166,7 @@
     back = exchange(best.reshape(CLUSTERS, 1, LANES)).reshape(CLUSTERS, LANES)
     out = pl.pallas_call(
         unpack, out_shape=shape((1, rows), f32), in_specs=[VMEM, VMEM], name="unpack"
-    )(on_chip(back), target)
+    )(on_chip(back), on_chip(target))
     return out.reshape(rows)
 
 

time: 88.7 us -> 85.5 us (0.964)
  Pallas kernels: 8.71 us -> 5.86 us
    pallas_call x1, Pallas kernels: 5.03 us -> 2.84 us  [shards(): pl.pallas_call(pack, out_shape=(pltpu.VMEM((CLUSTERS, 2, wide), bf16), pl...]
where the time goes in v2:
time: 85.5 us; the launch traced here: 85.4 us
  blocking collectives  79.5 us (93%)
  Pallas kernels  5.86 us (7%)
    all_to_all x2, blocking collectives, exchange(): return lax.all_to_all(x, AXES, 0, 0, tiled=True)  79.5 us
    pallas_call x1, Pallas kernels, shards(): pl.pallas_call(pack, out_shape=(pltpu.VMEM((CLUSTERS, 2, wide), bf16), pl...  2.84 us
    pallas_call x1, Pallas kernels, shards(): pl.pallas_call(score, out_shape=pltpu.VMEM((CLUSTERS, LANES), f32), in_sp...  2.14 us

profile of v2, /device:TPU:1, one launch (start us, length us, event | category | flops | bytes accessed | tf_op | source)
XLA Modules:
  0.0 85.4 jit_solution(10440643314031783807)
XLA Ops:
  0.0 2.8 %pack.1 = (bf16[256,2,1664]{2,1,0:T(2,128)(2,1)S(1)}, s32[1,512]{1,0:T(1,128)S(1)}) custom-call(s32[1,512]{1,0:T(1,128)} %bitcast.9, s32[1,512]{1,0:T(1,128)} %bitcast.10, bf16[512,768]{1,0:T(8,128)(2,1)} %rows_hbm.1), custom_call_target="tpu_custom_call" | custom-call | tf_op jit(solution)/shard_map/pack/pallas_call | solution.py:142
  2.9 60.4 %all_to_all.10.rows_ref = bf16[256,2,1664]{2,1,0:T(2,128)(2,1)S(1)} all-to-all(bf16[256,2,1664]{2,1,0:T(2,128)(2,1)S(1)} %get-tuple-element.7), channel_id=1, replica_groups=mesh['loader'=64,'split'=4] {'loader','split'}, dimensions={0} | all-to-all | bytes 3407872 | tf_op jit(solution)/shard_map/all_to_all | solution.py:133
  63.3 2.1 %score.1 = f32[256,128]{1,0:T(8,128)S(1)} custom-call(bf16[256,2,1664]{2,1,0:T(2,128)(2,1)S(1)} %all_to_all.10.rows_ref), custom_call_target="tpu_custom_call" | custom-call | tf_op jit(solution)/shard_map/score/pallas_call | solution.py:158
  65.4 19.1 %all_to_all.11 = f32[256,1,128]{2,1,0:T(1,128)S(1)} all-to-all(f32[256,1,128]{2,1,0:T(1,128)S(1)} %bitcast.7), channel_id=1, replica_groups=mesh['loader'=64,'split'=4] {'loader','split'}, dimensions={0} | all-to-all | bytes 262144 | tf_op jit(solution)/shard_map/all_to_all | solution.py:133
  84.5 0.9 %unpack.1 = f32[1,512]{1,0:T(1,128)} custom-call(f32[256,128]{1,0:T(8,128)S(1)} %bitcast.8, s32[1,512]{1,0:T(1,128)S(1)} %get-tuple-element.8.target_ref), custom_call_target="tpu_custom_call" | custom-call | tf_op jit(solution)/shard_map/unpack/pallas_call | solution.py:167

commit v3 on v2

--- a/solution.py
+++ b/solution.py
@@ -9,8 +9,9 @@
 CAP = 4
 LANES = 128
 BLOCKS = 4
-CHUNKS = 4
+CHUNKS = 2
 DIGIT = 64
+TILE = 256
 AXES = ("loader", "split")
 VMEM = pl.BlockSpec(memory_space=pltpu.VMEM)
 
@@ -80,30 +81,53 @@
     sources, _, wide = rows_ref.shape
     slots, width = keys_ref.shape
     half = slots // 2
-    block = 256
     keys_ref[:half, :] = rows_ref[:, :, :width].reshape(half, width)
     keys_ref[half:, :] = rows_ref[:, :, width : 2 * width].reshape(half, width)
     digits = rows_ref[:, :, 2 * width :].reshape(half, LANES)
+
     def weights(dims, dim, other, size):
         place = iota(dims, dim) - 3 * (iota(dims, other) // size)
         value = jnp.where(place == 0, DIGIT * DIGIT, jnp.where(place == 1, DIGIT, jnp.where(place == 2, 1, 0)))
         return value.astype(jnp.float32).astype(jnp.bfloat16)
-    column = dot(digits, weights((LANES, 2 * LANES), 0, 1, LANES))
-    row = dot(weights((8, LANES), 1, 0, 1), digits, 1)
-    row = jnp.where(row == 0.0, 1e9, row)
-    keys = keys_ref[...]
-    for q in range(slots // block):
-        scores = dot(keys_ref[q * block : (q + 1) * block, :], keys, 1)
-        side, start = divmod(q * block, half)
-        query_rank = column[start : start + block, side * LANES : (side + 1) * LANES]
-        best = jnp.full((block, LANES), -1.0, jnp.float32)
-        for k in range(slots // LANES):
-            part = k * LANES
-            key_rank = row[part // half : part // half + 1, part % half : part % half + LANES]
-            allowed = key_rank < query_rank
-            best = jnp.maximum(best, jnp.where(allowed, scores[:, part : part + LANES], -1.0))
-        best_ref[q * block : (q + 1) * block, :] = jnp.broadcast_to(
-            jnp.max(best, axis=1, keepdims=True), (block, LANES)
+
+    def settled(rank):
+        return jnp.where(rank == 0.0, 1e9, rank)
+
+    column = settled(dot(digits, weights((LANES, 2 * LANES), 0, 1, LANES)))
+    row = settled(dot(weights((8, LANES), 1, 0, 1), digits, 1))
+    count = slots // TILE
+    parts = TILE // LANES
+
+    def down(block):
+        side, start = divmod(block * TILE, half)
+        return column[start : start + TILE, side * LANES : (side + 1) * LANES]
+
+    def across(block, part):
+        side, start = divmod(block * TILE + part * LANES, half)
+        return row[side : side + 1, start : start + LANES]
+
+    diagonal = iota((LANES, LANES), 0) == iota((LANES, LANES), 1)
+    best = [jnp.full((TILE, LANES), -1.0, jnp.float32)] * count
+    for j in range(count):
+        top = [jnp.full((8, LANES), -1.0, jnp.float32)] * parts
+        for i in range(j + 1):
+            scores = dot(keys_ref[i * TILE : (i + 1) * TILE, :], keys_ref[j * TILE : (j + 1) * TILE, :], 1)
+            for part in range(parts):
+                piece = scores[:, part * LANES : (part + 1) * LANES]
+                allowed = across(j, part) < down(i)
+                best[i] = jnp.maximum(best[i], jnp.where(allowed, piece, -1.0))
+                if i < j:
+                    other = jnp.where(allowed, -1.0, piece).reshape(TILE // 8, 8, LANES)
+                    top[part] = jnp.maximum(top[part], jnp.max(other, axis=0))
+        if j > 0:
+            extra = [
+                jnp.where(diagonal, jnp.max(top[part], axis=0, keepdims=True), -1.0)
+                for part in range(parts)
+            ]
+            best[j] = jnp.maximum(best[j], jnp.concatenate(extra, axis=0))
+    for i in range(count):
+        best_ref[i * TILE : (i + 1) * TILE, :] = jnp.broadcast_to(
+            jnp.max(best[i], axis=1, keepdims=True), (TILE, LANES)
         )
     lane = iota((sources, LANES), 1)
     out = best_ref[pl.ds(0, sources, stride=2), :]

time: 85.5 us -> 84.8 us (level)
  no operation moved by 1% of the time
where the time goes in v3:
time: 84.8 us; the launch traced here: 84.6 us
  blocking collectives  79.5 us (94%)
  Pallas kernels  5.12 us (6%)
    all_to_all x2, blocking collectives, exchange(): return lax.all_to_all(x, AXES, 0, 0, tiled=True)  79.5 us
    pallas_call x1, Pallas kernels, shards(): pl.pallas_call(pack, out_shape=(pltpu.VMEM((CLUSTERS, 2, wide), bf16), pl...  2.66 us

profile of v3, /device:TPU:1, one launch (start us, length us, event | category | flops | bytes accessed | tf_op | source)
XLA Modules:
  0.0 84.6 jit_solution(4187763905899435055)
XLA Ops:
  0.0 2.7 %pack.1 = (bf16[256,2,1664]{2,1,0:T(2,128)(2,1)S(1)}, s32[1,512]{1,0:T(1,128)S(1)}) custom-call(s32[1,512]{1,0:T(1,128)} %bitcast.9, s32[1,512]{1,0:T(1,128)} %bitcast.10, bf16[512,768]{1,0:T(8,128)(2,1)} %rows_hbm.1), custom_call_target="tpu_custom_call" | custom-call | tf_op jit(solution)/shard_map/pack/pallas_call | solution.py:166
  2.7 60.4 %all_to_all.10.rows_ref = bf16[256,2,1664]{2,1,0:T(2,128)(2,1)S(1)} all-to-all(bf16[256,2,1664]{2,1,0:T(2,128)(2,1)S(1)} %get-tuple-element.7), channel_id=1, replica_groups=mesh['loader'=64,'split'=4] {'loader','split'}, dimensions={0} | all-to-all | bytes 3407872 | tf_op jit(solution)/shard_map/all_to_all | solution.py:157
  63.1 1.6 %score.1 = f32[256,128]{1,0:T(8,128)S(1)} custom-call(bf16[256,2,1664]{2,1,0:T(2,128)(2,1)S(1)} %all_to_all.10.rows_ref), custom_call_target="tpu_custom_call" | custom-call | tf_op jit(solution)/shard_map/score/pallas_call | solution.py:182
  64.7 19.1 %all_to_all.11 = f32[256,1,128]{2,1,0:T(1,128)S(1)} all-to-all(f32[256,1,128]{2,1,0:T(1,128)S(1)} %bitcast.7), channel_id=1, replica_groups=mesh['loader'=64,'split'=4] {'loader','split'}, dimensions={0} | all-to-all | bytes 262144 | tf_op jit(solution)/shard_map/all_to_all | solution.py:157
  83.8 0.9 %unpack.1 = f32[1,512]{1,0:T(1,128)} custom-call(f32[256,128]{1,0:T(8,128)S(1)} %bitcast.8, s32[1,512]{1,0:T(1,128)S(1)} %get-tuple-element.8.target_ref), custom_call_target="tpu_custom_call" | custom-call | tf_op jit(solution)/shard_map/unpack/pallas_call | solution.py:191

commit v4 on v2

v4 whole, which is shorter than its diff:
```python
import jax
import jax.numpy as jnp
from jax import lax
from jax.experimental import pallas as pl
from jax.experimental.pallas import tpu as pltpu
from jax.sharding import Mesh, PartitionSpec as P

CLUSTERS = 256
CHIPS = 128
CAP = 4
LANES = 128
CHUNKS = 2
DIGIT = 64
DIGITS = 3
TILE = 256
FAR = (4, 2, 2)
AXES = "d"
VMEM = pl.BlockSpec(memory_space=pltpu.VMEM)
HBM = pl.BlockSpec(memory_space=pltpu.HBM)
LIMIT = pltpu.CompilerParams(vmem_limit_bytes=16 << 20)

epsilon = 1e-06


def flat(z, x, y, core):
    return ((z * 4 + x) * 2 + core) * 4 + y


def chip_order():
    chips = [(z, x, y) for z in range(8) for x in range(4) for y in range(4)]
    return [FAR] + [chip for chip in chips if chip != FAR]


CORES = [[flat(*chip, core) for chip in chip_order()] for core in range(2)]
PARTNER = [(flat(*chip, core), flat(*chip, 1 - core)) for chip in chip_order() for core in range(2)]


def this_core():
    return lax.axis_index(AXES) // 4 % 2


def iota(dims, dim):
    return lax.broadcasted_iota(jnp.int32, dims, dim)


def flag(mask):
    return mask.astype(jnp.float32).astype(jnp.bfloat16)


def dot(a, b, contract_b=0):
    return lax.dot_general(
        a, b, (((1,), (contract_b,)), ((), ())), preferred_element_type=jnp.float32
    )


def pack(ids_hbm, rank_hbm, rows_hbm, out_ref, target_ref, ids_ref, rank_ref, held, unit_ref, digit_ref, sems):
    rows, width = held.shape
    chunk = rows // CHUNKS
    loads = [
        pltpu.make_async_copy(ids_hbm, ids_ref, sems.at[0]),
        pltpu.make_async_copy(rank_hbm, rank_ref, sems.at[1]),
    ]
    for c in range(CHUNKS):
        part = pl.ds(c * chunk, chunk)
        loads.append(pltpu.make_async_copy(rows_hbm.at[part], held.at[part], sems.at[2 + c]))
    for load in loads:
        load.start()
    loads[0].wait()
    loads[1].wait()
    cluster = ids_ref[...]
    member = iota((CLUSTERS, rows), 0) == cluster
    before = iota((rows, rows), 0) < iota((rows, rows), 1)
    count = dot(flag(member), flag(before))
    position = jnp.sum(jnp.where(member, count, 0.0), axis=0, keepdims=True).astype(jnp.int32)
    chip, core = cluster // 2, cluster % 2
    other = jnp.where(core == this_core(), 0, 1)
    target_ref[...] = (chip * 2 + other) * CAP + position
    slot = ((other * 2 + position // 2) * CHIPS + chip) * 2 + position % 2
    rank = rank_ref[...] + 1
    which = iota((LANES, rows), 0) % DIGITS
    high, middle, low = rank // (DIGIT * DIGIT), rank // DIGIT % DIGIT, rank % DIGIT
    digits = jnp.where(which == 0, high, jnp.where(which == 1, middle, low))
    digit_ref[...] = digits.astype(jnp.float32).astype(jnp.bfloat16)
    for c in range(CHUNKS):
        loads[2 + c].wait()
        values = held[c * chunk : (c + 1) * chunk, :].astype(jnp.float32)
        scale = lax.rsqrt(jnp.sum(values * values, axis=1, keepdims=True) + epsilon)
        unit_ref[c * chunk : (c + 1) * chunk, :] = (values * scale).astype(jnp.bfloat16)
    pairs = 2 * CHIPS
    group = iota((pairs, LANES), 1) // DIGITS
    ranks = jnp.zeros((pairs, LANES), jnp.float32)
    for b in range(CAP):
        pick = flag(iota((pairs, rows), 0) + b * pairs == slot)
        packed = dot(pick, unit_ref[...]).astype(jnp.bfloat16)
        out_ref[:, :, b * width : (b + 1) * width] = packed.reshape(CHIPS, 2, width)
        ranks = jnp.where(group == b, dot(pick, digit_ref[...], 1), ranks)
    out_ref[:, :, CAP * width :] = ranks.astype(jnp.bfloat16).reshape(CHIPS, 2, LANES)


def hand(rows_ref, out_ref):
    chips, _, wide = rows_ref.shape
    pairs = 2 * chips
    width = (wide - LANES) // CAP
    for u in range(2):
        place = slice(u * pairs, (u + 1) * pairs)
        start = (2 + u) * width
        out_ref[place, :width] = rows_ref[:, :, start : start + width].reshape(pairs, width)
        out_ref[place, width:] = rows_ref[:, :, CAP * width :].reshape(pairs, LANES)


def weights(dims, dim, b):
    place = iota(dims, dim) - DIGITS * b
    value = jnp.where(place == 0, DIGIT * DIGIT, jnp.where(place == 1, DIGIT, jnp.where(place == 2, 1, 0)))
    return value.astype(jnp.float32).astype(jnp.bfloat16)


def settled(rank):
    return jnp.where(rank == 0.0, 1e9, rank)


def ranks_of(digits, b):
    down = settled(dot(digits, weights((LANES, LANES), 0, b)))
    return down, settled(dot(weights((8, LANES), 1, b), digits, 1))


def blocks_of(ref):
    return [ref[u * TILE : (u + 1) * TILE, :] for u in range(2)]


def raise_best(best, keys, down, across, pairs):
    parts = TILE // LANES
    diagonal = iota((LANES, LANES), 0) == iota((LANES, LANES), 1)
    for j in sorted({j for _, j in pairs}):
        top = [jnp.full((8, LANES), -1.0, jnp.float32)] * parts
        for i in [i for i, other in pairs if other == j]:
            scores = dot(keys[i], keys[j], 1)
            for part in range(parts):
                place = slice(part * LANES, (part + 1) * LANES)
                piece = scores[:, place]
                allowed = across[j][0:1, place] < down[i]
                best[i] = jnp.maximum(best[i], jnp.where(allowed, piece, -1.0))
                if i != j:
                    rest = jnp.where(allowed, -1.0, piece).reshape(TILE // 8, 8, LANES)
                    top[part] = jnp.maximum(top[part], jnp.max(rest, axis=0))
        extra = [jnp.where(diagonal, jnp.max(t, axis=0, keepdims=True), -1.0) for t in top]
        best[j] = jnp.maximum(best[j], jnp.concatenate(extra, axis=0))


def score_own(rows_ref, keys_ref, down_ref, across_ref, best_ref):
    _, _, wide = rows_ref.shape
    _, width = keys_ref.shape
    digits = rows_ref[:, :, CAP * width :].reshape(TILE, LANES)
    down, across = zip(*[ranks_of(digits, b) for b in range(2)])
    for u in range(2):
        place = slice(u * TILE, (u + 1) * TILE)
        keys_ref[place, :] = rows_ref[:, :, u * width : (u + 1) * width].reshape(TILE, width)
        down_ref[place, :] = down[u]
        across_ref[u * 8 : (u + 1) * 8, :] = across[u]
    best = [jnp.full((TILE, LANES), -1.0, jnp.float32)] * 2
    raise_best(best, blocks_of(keys_ref), down, across, [(0, 0), (0, 1), (1, 1)])
    for u in range(2):
        best_ref[u * TILE : (u + 1) * TILE, :] = best[u]


def score(own_ref, down_ref, across_ref, start_ref, got_ref, digit_ref, mine_ref, theirs_ref, best_ref):
    half, _ = own_ref.shape
    chips = half // CAP
    down, across = blocks_of(down_ref), [across_ref[u * 8 : (u + 1) * 8, :] for u in range(2)]
    for u, digits in enumerate(blocks_of(digit_ref)):
        column, row = ranks_of(digits, 2 + u)
        down.append(column)
        across.append(row)
    best = blocks_of(start_ref) + [jnp.full((TILE, LANES), -1.0, jnp.float32)] * 2
    pairs = [(0, 2), (1, 2), (2, 2), (0, 3), (1, 3), (2, 3), (3, 3)]
    raise_best(best, blocks_of(own_ref) + blocks_of(got_ref), down, across, pairs)
    for i in range(CAP):
        best_ref[i * TILE : (i + 1) * TILE, :] = jnp.broadcast_to(
            jnp.max(best[i], axis=1, keepdims=True), (TILE, LANES)
        )
    lane = iota((chips, LANES), 1)
    for other, ref in enumerate((mine_ref, theirs_ref)):
        out = jnp.full((chips, LANES), -jnp.inf, jnp.float32)
        for p in range(CAP):
            start = (2 * other + p // 2) * TILE + p % 2
            out = jnp.where(lane == CAP * other + p, best_ref[pl.ds(start, chips, stride=2), :], out)
        ref[...] = out


def unpack(back_ref, target_ref, out_ref):
    rows = target_ref.shape[1]
    back = back_ref[...]
    target = target_ref[...]
    place = target % (2 * CAP)
    value = jnp.zeros((CHIPS, rows), jnp.float32)
    for p in range(2 * CAP):
        value = jnp.where(place == p, jnp.broadcast_to(back[:, p : p + 1], (CHIPS, rows)), value)
    member = iota((CHIPS, rows), 0) == target // (2 * CAP)
    out_ref[...] = jnp.sum(jnp.where(member, value, 0.0), axis=0, keepdims=True)


def on_chip(x):
    return pltpu.with_memory_space_constraint(x, pltpu.VMEM)


def off_chip(x):
    return pltpu.with_memory_space_constraint(x, pltpu.HBM)


def exchange(x, groups):
    return lax.all_to_all(x, AXES, 0, 0, axis_index_groups=groups, tiled=True)


def swap(x):
    return lax.ppermute(x, AXES, PARTNER)


def shards(embeddings, cluster_ids, ranks):
    rows, width = embeddings.shape
    slots = CLUSTERS * CAP
    wide = CAP * width + LANES
    f32, i32, bf16 = jnp.float32, jnp.int32, jnp.bfloat16
    packed, target = pl.pallas_call(
        pack,
        out_shape=(pltpu.VMEM((CHIPS, 2, wide), bf16), pltpu.VMEM((1, rows), i32)),
        in_specs=[HBM] * 3,
        out_specs=(VMEM, VMEM),
        scratch_shapes=[
            pltpu.VMEM((1, rows), i32),
            pltpu.VMEM((1, rows), i32),
            pltpu.VMEM((rows, width), bf16),
            pltpu.VMEM((rows, width), bf16),
            pltpu.VMEM((LANES, rows), bf16),
            pltpu.SemaphoreType.DMA((2 + CHUNKS,)),
        ],
        compiler_params=LIMIT,
        name="pack",
    )(*map(off_chip, (cluster_ids.reshape(1, rows), ranks.reshape(1, rows), embeddings)))
    arrived = on_chip(exchange(packed, CORES))
    given = pl.pallas_call(
        hand,
        out_shape=pltpu.VMEM((slots // 2, width + LANES), bf16),
        in_specs=[VMEM],
        out_specs=VMEM,
        compiler_params=LIMIT,
        name="hand",
    )(arrived)
    with jax.named_scope("swap"):
        got = swap(given)
    half = slots // 2
    own, down, across, begun = pl.pallas_call(
        score_own,
        out_shape=(
            pltpu.VMEM((half, width), bf16),
            pltpu.VMEM((half, LANES), f32),
            pltpu.VMEM((16, TILE), f32),
            pltpu.VMEM((half, LANES), f32),
        ),
        in_specs=[VMEM],
        out_specs=(VMEM,) * 4,
        compiler_params=LIMIT,
        name="score_own",
    )(arrived)
    mine, theirs = pl.pallas_call(
        score,
        out_shape=(pltpu.VMEM((CHIPS, LANES), f32),) * 2,
        in_specs=[VMEM] * 6,
        out_specs=(VMEM, VMEM),
        scratch_shapes=[pltpu.VMEM((slots, LANES), f32)],
        compiler_params=LIMIT,
        name="score",
    )(*map(on_chip, (own, down, across, begun, got[:, :width], got[:, width:])))
    best = jnp.maximum(mine, swap(theirs))
    back = exchange(best.reshape(CHIPS, 1, LANES), CORES).reshape(CHIPS, LANES)
    out = pl.pallas_call(
        unpack,
        out_shape=jax.ShapeDtypeStruct((1, rows), f32),
        in_specs=[VMEM] * 2,
        compiler_params=LIMIT,
        name="unpack",
    )(*map(on_chip, (back, target)))
    return out.reshape(rows)


def solution(mesh):
    line = Mesh(mesh.devices.reshape(-1), (AXES,))
    return jax.shard_map(
        shards,
        mesh=line,
        in_specs=(P(AXES, None), P(AXES, None), P(AXES)),
        out_specs=P(AXES),
        check_vma=False,
    )
```

time: 85.5 us -> 79.7 us (0.932)
  blocking collectives: 79.5 us -> 69.6 us
  waiting for transfers between devices: 0 us -> 2.39 us
  starting transfers between devices: 0 us -> 1.74 us
    all_to_all x2, blocking collectives: 79.5 us -> 69.6 us  [exchange(): return lax.all_to_all(x, AXES, 0, 0, axis_index_groups=groups, tiled=True)]
    ppermute x0 -> x2, waiting for transfers between devices: none -> 2.39 us  [swap(): return lax.ppermute(x, AXES, PARTNER)]
    ppermute x0 -> x2, starting transfers between devices: none -> 1.74 us  [swap(): return lax.ppermute(x, AXES, PARTNER)]
    pallas_call x3 -> x5, Pallas kernels: 5.86 us -> 5.48 us  [the longest x1 2.69 us: shards(): pl.pallas_call(pack, out_shape=(pltpu.VMEM((CHIPS, 2, wide), bf16), pltpu...]
  transfers between devices with their start and end apart: 0 -> 2, of which waited for: 0 -> 2; matrix products, arithmetic and copies ran while one was open for 0% -> 0% of each run, Pallas kernels for 0% -> 1%
where the time goes in v4:
time: 79.7 us; the launch traced here: 79.3 us
  blocking collectives  69.6 us (87%)
  Pallas kernels  5.48 us (7%)
  waiting for transfers between devices  2.39 us (3%)
  starting transfers between devices  1.74 us (2%)
    all_to_all x2, blocking collectives, exchange(): return lax.all_to_all(x, AXES, 0, 0, axis_index_groups=groups, tiled=True)  69.6 us
    pallas_call x1, Pallas kernels, shards(): pl.pallas_call(pack, out_shape=(pltpu.VMEM((CHIPS, 2, wide), bf16), pltpu...  2.69 us
    ppermute x2, waiting for transfers between devices, swap(): return lax.ppermute(x, AXES, PARTNER)  2.39 us
    ppermute x2, starting transfers between devices, swap(): return lax.ppermute(x, AXES, PARTNER)  1.74 us
  transfers between devices with their start and end apart: 2, of which 2 were waited for; matrix products, arithmetic and copies ran while one was open for 0% of the time, Pallas kernels for 1%

profile of v4, /device:TPU:1, one launch (start us, length us, event | category | flops | bytes accessed | tf_op | source)
XLA Modules:
  0.0 79.3 jit_solution(18357548127815937405)
XLA Ops:
  0.0 2.7 %pack.1 = (bf16[128,2,3200]{2,1,0:T(2,128)(2,1)S(1)}, s32[1,512]{1,0:T(1,128)S(1)}) custom-call(s32[1,512]{1,0:T(1,128)} %bitcast.9, s32[1,512]{1,0:T(1,128)} %bitcast.10, bf16[512,768]{1,0:T(8,128)(2,1)} %rows_hbm.1), custom_call_target="tpu_custom_call" | custom-call | tf_op jit(solution)/shard_map/pack/pallas_call | solution.py:222
  2.7 53.3 %all_to_all.10.rows_ref = bf16[128,2,3200]{2,1,0:T(2,128)(2,1)S(1)} all-to-all(bf16[128,2,3200]{2,1,0:T(2,128)(2,1)S(1)} %get-tuple-element.13), channel_id=1, replica_groups={{146,0,1,2,3,8,9,10,11,16,17,18,19,24,25,26,27,32,33,34,35,40,41,42,43,..., dimensions={0} | all-to-all | bytes 3276800 | tf_op jit(solution)/shard_map/all_to_all | solution.py:210
  56.0 0.2 hand.1
  56.2 1.3 %collective-permute-start = (bf16[512,896]{1,0:T(8,128)(2,1)S(1)}, bf16[512,896]{1,0:T(8,128)(2,1)S(1)}, u32[]{:S(2)}, u32[]{:S(2)}) collective-permute-start(bf16[512,896]{1,0:T(8,128)(2,1)S(1)} %hand.1), channel_id=1, source_target_pairs={{146,150},{150,146},{0,4},{4,0},{1,5},{5,1},{2,6},{6,2},{3,7},{7,3... | collective-permute-start | bytes 2752520 | tf_op jit(solution)/shard_map/swap/ppermute | solution.py:214
  57.5 0.6 score_own.1
  58.1 1.5 %collective-permute-done = bf16[512,896]{1,0:T(8,128)(2,1)S(1)} collective-permute-done((bf16[512,896]{1,0:T(8,128)(2,1)S(1)}, bf16[512,896]{1,0:T(8,128)(2,1)S(1)}, u32[]{:S(2)}, u32[]{:S(2)}) %collective-permute-start) | collective-permute-done | bytes 917536 | tf_op jit(solution)/shard_map/swap/ppermute | solution.py:214
  59.6 0.1 slice.8.got_ref
  59.6 1.1 %score.1 = (f32[128,128]{1,0:T(8,128)S(1)}, f32[128,128]{1,0:T(8,128)S(1)}) custom-call(bf16[512,768]{1,0:T(8,128)(2,1)S(1)} %get-tuple-element.14.own_ref, f32[512,128]{1,0:T(8,128)S(1)} %get-tuple-element.15.down_ref, f32[16,256]{1,0:T(8,128)S(1)} %get-tuple-element.16.across_ref, f32[512,128]{1,0:T(8,128)S(1)} %get-tuple-element.17.start_ref, ...), custom_call_target="tpu_custom_call" | custom-call | tf_op jit(solution)/shard_map/score/pallas_call | solution.py:263
  60.8 0.5 collective-permute-start.1
  61.2 0.9 %collective-permute-done.1 = f32[128,128]{1,0:T(8,128)S(1)} collective-permute-done((f32[128,128]{1,0:T(8,128)S(1)}, f32[128,128]{1,0:T(8,128)S(1)}, u32[]{:S(2)}, u32[]{:S(2)}) %collective-permute-start.1) | collective-permute-done | bytes 65568 | tf_op jit(solution)/shard_map/ppermute | solution.py:214
  62.2 16.3 %all_to_all.11 = f32[128,1,128]{2,1,0:T(1,128)S(1)} all-to-all(f32[128,1,128]{2,1,0:T(1,128)S(1)} %bitcast.8), channel_id=1, replica_groups={{146,0,1,2,3,8,9,10,11,16,17,18,19,24,25,26,27,32,33,34,35,40,41,42,43,..., dimensions={0} | all-to-all | bytes 131072 | tf_op jit(solution)/shard_map/all_to_all | solution.py:210
  78.5 0.9 %unpack.1 = f32[1,512]{1,0:T(1,128)} custom-call(f32[128,128]{1,0:T(8,128)S(1)} %bitcast.7, s32[1,512]{1,0:T(1,128)S(1)} %get-tuple-element.20.target_ref), custom_call_target="tpu_custom_call" | custom-call | tf_op jit(solution)/shard_map/unpack/pallas_call | solution.py:274
  (2 shorter events, 0.0 us)
Async XLA Ops:
  56.2 3.4 %collective-permute-start = (bf16[512,896]{1,0:T(8,128)(2,1)S(1)}, bf16[512,896]{1,0:T(8,128)(2,1)S(1)}, u32[]{:S(2)}, u32[]{:S(2)}) collective-permute-start(bf16[512,896]{1,0:T(8,128)(2,1)S(1)} %hand.1), channel_id=1, source_target_pairs={{146,150},{150,146},{0,4},{4,0},{1,5},{5,1},{2,6},{6,2},{3,7},{7,3... | collective-permute-start | bytes 2752520 | tf_op jit(solution)/shard_map/swap/ppermute | solution.py:214
  60.8 1.4 %collective-permute-start.1 = (f32[128,128]{1,0:T(8,128)S(1)}, f32[128,128]{1,0:T(8,128)S(1)}, u32[]{:S(2)}, u32[]{:S(2)}) collective-permute-start(f32[128,128]{1,0:T(8,128)S(1)} %get-tuple-element.19), channel_id=1, source_target_pairs={{146,150},{150,146},{0,4},{4,0},{1,5},{5,1},{2,6},{6,2},{3,7},{7,3... | collective-permute-start | bytes 196616 | tf_op jit(solution)/shard_map/ppermute | solution.py:214

commit v5 on v4

--- a/solution.py
+++ b/solution.py
@@ -13,7 +13,6 @@
 DIGIT = 64
 DIGITS = 3
 TILE = 256
-FAR = (4, 2, 2)
 AXES = "d"
 VMEM = pl.BlockSpec(memory_space=pltpu.VMEM)
 HBM = pl.BlockSpec(memory_space=pltpu.HBM)
@@ -26,13 +25,15 @@
     return ((z * 4 + x) * 2 + core) * 4 + y
 
 
-def chip_order():
-    chips = [(z, x, y) for z in range(8) for x in range(4) for y in range(4)]
-    return [FAR] + [chip for chip in chips if chip != FAR]
-
-
-CORES = [[flat(*chip, core) for chip in chip_order()] for core in range(2)]
-PARTNER = [(flat(*chip, core), flat(*chip, 1 - core)) for chip in chip_order() for core in range(2)]
+OUT_LEAD, BACK_LEAD = (5, 2, 3), (4, 2, 2)
+CHIP_LIST = [(z, x, y) for z in range(8) for x in range(4) for y in range(4)]
+OUT_CHIPS = [OUT_LEAD] + [chip for chip in CHIP_LIST if chip != OUT_LEAD]
+LEAD = OUT_CHIPS.index(BACK_LEAD)
+BACK_CHIPS = list(OUT_CHIPS)
+BACK_CHIPS[0], BACK_CHIPS[LEAD] = OUT_CHIPS[LEAD], OUT_CHIPS[0]
+OUT_GROUPS = [[flat(*chip, core) for chip in OUT_CHIPS] for core in range(2)]
+BACK_GROUPS = [[flat(*chip, core) for chip in BACK_CHIPS] for core in range(2)]
+PARTNER = [(flat(*chip, core), flat(*chip, 1 - core)) for chip in CHIP_LIST for core in range(2)]
 
 
 def this_core():
@@ -74,7 +75,8 @@
     position = jnp.sum(jnp.where(member, count, 0.0), axis=0, keepdims=True).astype(jnp.int32)
     chip, core = cluster // 2, cluster % 2
     other = jnp.where(core == this_core(), 0, 1)
-    target_ref[...] = (chip * 2 + other) * CAP + position
+    back = jnp.where(chip == 0, LEAD, jnp.where(chip == LEAD, 0, chip))
+    target_ref[...] = (back * 2 + other) * CAP + position
     slot = ((other * 2 + position // 2) * CHIPS + chip) * 2 + position % 2
     rank = rank_ref[...] + 1
     which = iota((LANES, rows), 0) % DIGITS
@@ -146,44 +148,47 @@
         best[j] = jnp.maximum(best[j], jnp.concatenate(extra, axis=0))
 
 
-def score_own(rows_ref, keys_ref, down_ref, across_ref, best_ref):
+def gather_best(best, best_ref, first):
+    for u in range(2):
+        best_ref[u * TILE : (u + 1) * TILE, :] = jnp.broadcast_to(
+            jnp.max(best[u], axis=1, keepdims=True), (TILE, LANES)
+        )
+    lane = iota((CHIPS, LANES), 1)
+    out = jnp.full((CHIPS, LANES), -1.0, jnp.float32)
+    for p in range(CAP):
+        start = p // 2 * TILE + p % 2
+        out = jnp.where(lane == first + p, best_ref[pl.ds(start, CHIPS, stride=2), :], out)
+    return out
+
+
+def score_here(rows_ref, given_ref, keys_ref, down_ref, begun_ref, out_ref, best_ref):
     _, _, wide = rows_ref.shape
     _, width = keys_ref.shape
     digits = rows_ref[:, :, CAP * width :].reshape(TILE, LANES)
-    down, across = zip(*[ranks_of(digits, b) for b in range(2)])
+    down, across = zip(*[ranks_of(digits, b) for b in range(CAP)])
     for u in range(2):
         place = slice(u * TILE, (u + 1) * TILE)
         keys_ref[place, :] = rows_ref[:, :, u * width : (u + 1) * width].reshape(TILE, width)
         down_ref[place, :] = down[u]
-        across_ref[u * 8 : (u + 1) * 8, :] = across[u]
-    best = [jnp.full((TILE, LANES), -1.0, jnp.float32)] * 2
-    raise_best(best, blocks_of(keys_ref), down, across, [(0, 0), (0, 1), (1, 1)])
-    for u in range(2):
-        best_ref[u * TILE : (u + 1) * TILE, :] = best[u]
-
-
-def score(own_ref, down_ref, across_ref, start_ref, got_ref, digit_ref, mine_ref, theirs_ref, best_ref):
-    half, _ = own_ref.shape
-    chips = half // CAP
-    down, across = blocks_of(down_ref), [across_ref[u * 8 : (u + 1) * 8, :] for u in range(2)]
-    for u, digits in enumerate(blocks_of(digit_ref)):
-        column, row = ranks_of(digits, 2 + u)
-        down.append(column)
-        across.append(row)
-    best = blocks_of(start_ref) + [jnp.full((TILE, LANES), -1.0, jnp.float32)] * 2
-    pairs = [(0, 2), (1, 2), (2, 2), (0, 3), (1, 3), (2, 3), (3, 3)]
-    raise_best(best, blocks_of(own_ref) + blocks_of(got_ref), down, across, pairs)
-    for i in range(CAP):
-        best_ref[i * TILE : (i + 1) * TILE, :] = jnp.broadcast_to(
-            jnp.max(best[i], axis=1, keepdims=True), (TILE, LANES)
-        )
-    lane = iota((chips, LANES), 1)
-    for other, ref in enumerate((mine_ref, theirs_ref)):
-        out = jnp.full((chips, LANES), -jnp.inf, jnp.float32)
-        for p in range(CAP):
-            start = (2 * other + p // 2) * TILE + p % 2
-            out = jnp.where(lane == CAP * other + p, best_ref[pl.ds(start, chips, stride=2), :], out)
-        ref[...] = out
+    keys = blocks_of(keys_ref) + [given_ref[u * TILE : (u + 1) * TILE, :width] for u in range(2)]
+    best = [jnp.full((TILE, LANES), -1.0, jnp.float32)] * CAP
+    raise_best(best, keys, down, across, [(0, 0), (0, 1), (1, 1)])
+    for u in range(2):
+        begun_ref[u * TILE : (u + 1) * TILE, :] = best[u]
+    raise_best(best, keys, down, across, [(2, 2), (2, 3), (3, 3)])
+    out_ref[...] = gather_best(best[2:], best_ref, CAP)
+
+
+def score_swapped(keys_ref, down_ref, begun_ref, here_ref, got_ref, digit_ref, mine_ref, theirs_ref, best_ref):
+    across = [None] * 2 + [ranks_of(digits, 2 + u)[1] for u, digits in enumerate(blocks_of(digit_ref))]
+    best = blocks_of(begun_ref) + [jnp.full((TILE, LANES), -1.0, jnp.float32)] * 2
+    pairs = [(0, 2), (1, 2), (0, 3), (1, 3)]
+    raise_best(best, blocks_of(keys_ref) + blocks_of(got_ref), blocks_of(down_ref), across, pairs)
+    mine = jnp.maximum(gather_best(best[:2], best_ref.at[0], 0), here_ref[...])
+    for ref, found in ((mine_ref, mine), (theirs_ref, gather_best(best[2:], best_ref.at[1], CAP))):
+        ref[...] = found
+        ref[0:1, :] = found[LEAD : LEAD + 1, :]
+        ref[LEAD : LEAD + 1, :] = found[0:1, :]
 
 
 def unpack(back_ref, target_ref, out_ref):
@@ -235,7 +240,7 @@
         compiler_params=LIMIT,
         name="pack",
     )(*map(off_chip, (cluster_ids.reshape(1, rows), ranks.reshape(1, rows), embeddings)))
-    arrived = on_chip(exchange(packed, CORES))
+    arrived = on_chip(exchange(packed, OUT_GROUPS))
     given = pl.pallas_call(
         hand,
         out_shape=pltpu.VMEM((slots // 2, width + LANES), bf16),
@@ -247,30 +252,31 @@
     with jax.named_scope("swap"):
         got = swap(given)
     half = slots // 2
-    own, down, across, begun = pl.pallas_call(
-        score_own,
+    keys, down, begun, here = pl.pallas_call(
+        score_here,
         out_shape=(
             pltpu.VMEM((half, width), bf16),
             pltpu.VMEM((half, LANES), f32),
-            pltpu.VMEM((16, TILE), f32),
             pltpu.VMEM((half, LANES), f32),
+            pltpu.VMEM((CHIPS, LANES), f32),
         ),
-        in_specs=[VMEM],
+        in_specs=[VMEM] * 2,
         out_specs=(VMEM,) * 4,
-        compiler_params=LIMIT,
-        name="score_own",
-    )(arrived)
+        scratch_shapes=[pltpu.VMEM((half, LANES), f32)],
+        compiler_params=LIMIT,
+        name="score_here",
+    )(arrived, on_chip(given))
     mine, theirs = pl.pallas_call(
-        score,
+        score_swapped,
         out_shape=(pltpu.VMEM((CHIPS, LANES), f32),) * 2,
         in_specs=[VMEM] * 6,
         out_specs=(VMEM, VMEM),
-        scratch_shapes=[pltpu.VMEM((slots, LANES), f32)],
-        compiler_params=LIMIT,
-        name="score",
-    )(*map(on_chip, (own, down, across, begun, got[:, :width], got[:, width:])))
+        scratch_shapes=[pltpu.VMEM((2, half, LANES), f32)],
+        compiler_params=LIMIT,
+        name="score_swapped",
+    )(*map(on_chip, (keys, down, begun, here, got[:, :width], got[:, width:])))
     best = jnp.maximum(mine, swap(theirs))
-    back = exchange(best.reshape(CHIPS, 1, LANES), CORES).reshape(CHIPS, LANES)
+    back = exchange(best.reshape(CHIPS, 1, LANES), BACK_GROUPS).reshape(CHIPS, LANES)
     out = pl.pallas_call(
         unpack,
         out_shape=jax.ShapeDtypeStruct((1, rows), f32),

time: 79.7 us -> 78.4 us (0.984)
  blocking collectives: 69.6 us -> 68.3 us
    all_to_all x2, blocking collectives: 69.6 us -> 68.3 us  [exchange(): return lax.all_to_all(x, AXES, 0, 0, axis_index_groups=groups, tiled=True)]
where the time goes in v5:
time: 78.4 us; the launch traced here: 78.1 us
  blocking collectives  68.3 us (87%)
  Pallas kernels  5.68 us (7%)
  starting transfers between devices  2.1 us (3%)
  waiting for transfers between devices  1.88 us (2%)
    all_to_all x2, blocking collectives, exchange(): return lax.all_to_all(x, AXES, 0, 0, axis_index_groups=groups, tiled=True)  68.3 us
    pallas_call x1, Pallas kernels, shards(): pl.pallas_call(pack, out_shape=(pltpu.VMEM((CHIPS, 2, wide), bf16), pltpu...  2.69 us
    ppermute x2, starting transfers between devices, swap(): return lax.ppermute(x, AXES, PARTNER)  2.1 us
    ppermute x2, waiting for transfers between devices, swap(): return lax.ppermute(x, AXES, PARTNER)  1.88 us
  transfers between devices with their start and end apart: 2, of which 2 were waited for; matrix products, arithmetic and copies ran while one was open for 0% of the time, Pallas kernels for 1%

profile of v5, /device:TPU:1, one launch (start us, length us, event | category | flops | bytes accessed | tf_op | source)
XLA Modules:
  0.0 78.1 jit_solution(6423759402693088400)
XLA Ops:
  0.0 2.7 %pack.1 = (bf16[128,2,3200]{2,1,0:T(2,128)(2,1)S(1)}, s32[1,512]{1,0:T(1,128)S(1)}) custom-call(s32[1,512]{1,0:T(1,128)} %bitcast.9, s32[1,512]{1,0:T(1,128)} %bitcast.10, bf16[512,768]{1,0:T(8,128)(2,1)} %rows_hbm.1), custom_call_target="tpu_custom_call" | custom-call | tf_op jit(solution)/shard_map/pack/pallas_call | solution.py:227
  2.7 53.3 %all_to_all.10.rows_ref = bf16[128,2,3200]{2,1,0:T(2,128)(2,1)S(1)} all-to-all(bf16[128,2,3200]{2,1,0:T(2,128)(2,1)S(1)} %get-tuple-element.13), channel_id=1, replica_groups={{179,0,1,2,3,8,9,10,11,16,17,18,19,24,25,26,27,32,33,34,35,40,41,42,43,..., dimensions={0} | all-to-all | bytes 3276800 | tf_op jit(solution)/shard_map/all_to_all | solution.py:215
  56.0 0.2 hand.1.given_ref
  56.2 1.6 %collective-permute-start = (bf16[512,896]{1,0:T(8,128)(2,1)S(1)}, bf16[512,896]{1,0:T(8,128)(2,1)S(1)}, u32[]{:S(2)}, u32[]{:S(2)}) collective-permute-start(bf16[512,896]{1,0:T(8,128)(2,1)S(1)} %hand.1.given_ref), channel_id=1, source_target_pairs={{0,4},{4,0},{1,5},{5,1},{2,6},{6,2},{3,7},{7,3},{8,12},{12,8},{9,1... | collective-permute-start | bytes 2752520 | tf_op jit(solution)/shard_map/swap/ppermute | solution.py:219
  57.8 1.1 %score_here.1 = (bf16[512,768]{1,0:T(8,128)(2,1)S(1)}, f32[512,128]{1,0:T(8,128)S(1)}, f32[512,128]{1,0:T(8,128)S(1)}, f32[128,128]{1,0:T(8,128)S(1)}) custom-call(bf16[128,2,3200]{2,1,0:T(2,128)(2,1)S(1)} %all_to_all.10.rows_ref, bf16[512,896]{1,0:T(8,128)(2,1)S(1)} %hand.1.given_ref), custom_call_target="tpu_custom_call" | custom-call | tf_op jit(solution)/shard_map/score_here/pallas_call | solution.py:255
  58.9 1.0 %collective-permute-done = bf16[512,896]{1,0:T(8,128)(2,1)S(1)} collective-permute-done((bf16[512,896]{1,0:T(8,128)(2,1)S(1)}, bf16[512,896]{1,0:T(8,128)(2,1)S(1)}, u32[]{:S(2)}, u32[]{:S(2)}) %collective-permute-start) | collective-permute-done | bytes 917536 | tf_op jit(solution)/shard_map/swap/ppermute | solution.py:219
  59.9 0.1 slice.8.got_ref
  60.0 0.8 %score_swapped.1 = (f32[128,128]{1,0:T(8,128)S(1)}, f32[128,128]{1,0:T(8,128)S(1)}) custom-call(bf16[512,768]{1,0:T(8,128)(2,1)S(1)} %get-tuple-element.14.keys_ref, f32[512,128]{1,0:T(8,128)S(1)} %get-tuple-element.15.down_ref, f32[512,128]{1,0:T(8,128)S(1)} %get-tuple-element.16.begun_ref, f32[128,128]{1,0:T(8,128)S(1)} %get-tuple-element.17.here_ref, ...), custom_call_target="tpu_custom_call" | custom-call | tf_op jit(solution)/shard_map/score_swapped/pallas_call | solution.py:269
  60.8 0.5 collective-permute-start.1
  61.3 0.9 %collective-permute-done.1 = f32[128,128]{1,0:T(8,128)S(1)} collective-permute-done((f32[128,128]{1,0:T(8,128)S(1)}, f32[128,128]{1,0:T(8,128)S(1)}, u32[]{:S(2)}, u32[]{:S(2)}) %collective-permute-start.1) | collective-permute-done | bytes 65568 | tf_op jit(solution)/shard_map/ppermute | solution.py:219
  62.2 15.0 %all_to_all.11 = f32[128,1,128]{2,1,0:T(1,128)S(1)} all-to-all(f32[128,1,128]{2,1,0:T(1,128)S(1)} %bitcast.8), channel_id=1, replica_groups={{146,0,1,2,3,8,9,10,11,16,17,18,19,24,25,26,27,32,33,34,35,40,41,42,43,..., dimensions={0} | all-to-all | bytes 131072 | tf_op jit(solution)/shard_map/all_to_all | solution.py:215
  77.2 0.9 %unpack.1 = f32[1,512]{1,0:T(1,128)} custom-call(f32[128,128]{1,0:T(8,128)S(1)} %bitcast.7, s32[1,512]{1,0:T(1,128)S(1)} %get-tuple-element.20.target_ref), custom_call_target="tpu_custom_call" | custom-call | tf_op jit(solution)/shard_map/unpack/pallas_call | solution.py:280
  (2 shorter events, 0.0 us)
Async XLA Ops:
  56.2 3.7 %collective-permute-start = (bf16[512,896]{1,0:T(8,128)(2,1)S(1)}, bf16[512,896]{1,0:T(8,128)(2,1)S(1)}, u32[]{:S(2)}, u32[]{:S(2)}) collective-permute-start(bf16[512,896]{1,0:T(8,128)(2,1)S(1)} %hand.1.given_ref), channel_id=1, source_target_pairs={{0,4},{4,0},{1,5},{5,1},{2,6},{6,2},{3,7},{7,3},{8,12},{12,8},{9,1... | collective-permute-start | bytes 2752520 | tf_op jit(solution)/shard_map/swap/ppermute | solution.py:219
  60.8 1.4 %collective-permute-start.1 = (f32[128,128]{1,0:T(8,128)S(1)}, f32[128,128]{1,0:T(8,128)S(1)}, u32[]{:S(2)}, u32[]{:S(2)}) collective-permute-start(f32[128,128]{1,0:T(8,128)S(1)} %get-tuple-element.19), channel_id=1, source_target_pairs={{0,4},{4,0},{1,5},{5,1},{2,6},{6,2},{3,7},{7,3},{8,12},{12,8},{9,1... | collective-permute-start | bytes 196616 | tf_op jit(solution)/shard_map/ppermute | solution.py:219

commit v6 on v5

--- a/solution.py
+++ b/solution.py
@@ -90,12 +90,13 @@
         unit_ref[c * chunk : (c + 1) * chunk, :] = (values * scale).astype(jnp.bfloat16)
     pairs = 2 * CHIPS
     group = iota((pairs, LANES), 1) // DIGITS
+    pick = flag(iota((CAP * pairs, rows), 0) == slot)
+    packed = dot(pick, unit_ref[...]).astype(jnp.bfloat16)
+    digits = dot(pick, digit_ref[...], 1)
     ranks = jnp.zeros((pairs, LANES), jnp.float32)
     for b in range(CAP):
-        pick = flag(iota((pairs, rows), 0) + b * pairs == slot)
-        packed = dot(pick, unit_ref[...]).astype(jnp.bfloat16)
-        out_ref[:, :, b * width : (b + 1) * width] = packed.reshape(CHIPS, 2, width)
-        ranks = jnp.where(group == b, dot(pick, digit_ref[...], 1), ranks)
+        out_ref[:, :, b * width : (b + 1) * width] = packed[b * pairs : (b + 1) * pairs].reshape(CHIPS, 2, width)
+        ranks = jnp.where(group == b, digits[b * pairs : (b + 1) * pairs], ranks)
     out_ref[:, :, CAP * width :] = ranks.astype(jnp.bfloat16).reshape(CHIPS, 2, LANES)
 
 

time: 78.4 us -> 78.3 us (level)
  no operation moved by 1% of the time
where the time goes in v6:
time: 78.3 us; the launch traced here: 78 us
  blocking collectives  68.3 us (87%)
  Pallas kernels  5.61 us (7%)
  starting transfers between devices  2.1 us (3%)
  waiting for transfers between devices  1.88 us (2%)
    all_to_all x2, blocking collectives, exchange(): return lax.all_to_all(x, AXES, 0, 0, axis_index_groups=groups, tiled=True)  68.3 us
    pallas_call x1, Pallas kernels, shards(): pl.pallas_call(pack, out_shape=(pltpu.VMEM((CHIPS, 2, wide), bf16), pltpu...  2.61 us
    ppermute x2, starting transfers between devices, swap(): return lax.ppermute(x, AXES, PARTNER)  2.1 us
    ppermute x2, waiting for transfers between devices, swap(): return lax.ppermute(x, AXES, PARTNER)  1.88 us
  transfers between devices with their start and end apart: 2, of which 2 were waited for; matrix products, arithmetic and copies ran while one was open for 0% of the time, Pallas kernels for 1%

profile of v6, /device:TPU:1, one launch (start us, length us, event | category | flops | bytes accessed | tf_op | source)
XLA Modules:
  0.0 78.0 jit_solution(10371767131887782479)
XLA Ops:
  0.0 2.6 %pack.1 = (bf16[128,2,3200]{2,1,0:T(2,128)(2,1)S(1)}, s32[1,512]{1,0:T(1,128)S(1)}) custom-call(s32[1,512]{1,0:T(1,128)} %bitcast.9, s32[1,512]{1,0:T(1,128)} %bitcast.10, bf16[512,768]{1,0:T(8,128)(2,1)} %rows_hbm.1), custom_call_target="tpu_custom_call" | custom-call | tf_op jit(solution)/shard_map/pack/pallas_call | solution.py:228
  2.6 53.3 %all_to_all.10.rows_ref = bf16[128,2,3200]{2,1,0:T(2,128)(2,1)S(1)} all-to-all(bf16[128,2,3200]{2,1,0:T(2,128)(2,1)S(1)} %get-tuple-element.13), channel_id=1, replica_groups={{179,0,1,2,3,8,9,10,11,16,17,18,19,24,25,26,27,32,33,34,35,40,41,42,43,..., dimensions={0} | all-to-all | bytes 3276800 | tf_op jit(solution)/shard_map/all_to_all | solution.py:216
  55.9 0.2 hand.1.given_ref
  56.1 1.6 %collective-permute-start = (bf16[512,896]{1,0:T(8,128)(2,1)S(1)}, bf16[512,896]{1,0:T(8,128)(2,1)S(1)}, u32[]{:S(2)}, u32[]{:S(2)}) collective-permute-start(bf16[512,896]{1,0:T(8,128)(2,1)S(1)} %hand.1.given_ref), channel_id=1, source_target_pairs={{0,4},{4,0},{1,5},{5,1},{2,6},{6,2},{3,7},{7,3},{8,12},{12,8},{9,1... | collective-permute-start | bytes 2752520 | tf_op jit(solution)/shard_map/swap/ppermute | solution.py:220
  57.7 1.1 %score_here.1 = (bf16[512,768]{1,0:T(8,128)(2,1)S(1)}, f32[512,128]{1,0:T(8,128)S(1)}, f32[512,128]{1,0:T(8,128)S(1)}, f32[128,128]{1,0:T(8,128)S(1)}) custom-call(bf16[128,2,3200]{2,1,0:T(2,128)(2,1)S(1)} %all_to_all.10.rows_ref, bf16[512,896]{1,0:T(8,128)(2,1)S(1)} %hand.1.given_ref), custom_call_target="tpu_custom_call" | custom-call | tf_op jit(solution)/shard_map/score_here/pallas_call | solution.py:256
  58.9 1.0 %collective-permute-done = bf16[512,896]{1,0:T(8,128)(2,1)S(1)} collective-permute-done((bf16[512,896]{1,0:T(8,128)(2,1)S(1)}, bf16[512,896]{1,0:T(8,128)(2,1)S(1)}, u32[]{:S(2)}, u32[]{:S(2)}) %collective-permute-start) | collective-permute-done | bytes 917536 | tf_op jit(solution)/shard_map/swap/ppermute | solution.py:220
  59.8 0.1 slice.8.got_ref
  59.9 0.8 %score_swapped.1 = (f32[128,128]{1,0:T(8,128)S(1)}, f32[128,128]{1,0:T(8,128)S(1)}) custom-call(bf16[512,768]{1,0:T(8,128)(2,1)S(1)} %get-tuple-element.14.keys_ref, f32[512,128]{1,0:T(8,128)S(1)} %get-tuple-element.15.down_ref, f32[512,128]{1,0:T(8,128)S(1)} %get-tuple-element.16.begun_ref, f32[128,128]{1,0:T(8,128)S(1)} %get-tuple-element.17.here_ref, ...), custom_call_target="tpu_custom_call" | custom-call | tf_op jit(solution)/shard_map/score_swapped/pallas_call | solution.py:270
  60.7 0.5 collective-permute-start.1
  61.2 0.9 %collective-permute-done.1 = f32[128,128]{1,0:T(8,128)S(1)} collective-permute-done((f32[128,128]{1,0:T(8,128)S(1)}, f32[128,128]{1,0:T(8,128)S(1)}, u32[]{:S(2)}, u32[]{:S(2)}) %collective-permute-start.1) | collective-permute-done | bytes 65568 | tf_op jit(solution)/shard_map/ppermute | solution.py:220
  62.1 15.0 %all_to_all.11 = f32[128,1,128]{2,1,0:T(1,128)S(1)} all-to-all(f32[128,1,128]{2,1,0:T(1,128)S(1)} %bitcast.8), channel_id=1, replica_groups={{146,0,1,2,3,8,9,10,11,16,17,18,19,24,25,26,27,32,33,34,35,40,41,42,43,..., dimensions={0} | all-to-all | bytes 131072 | tf_op jit(solution)/shard_map/all_to_all | solution.py:216
  77.1 0.9 %unpack.1 = f32[1,512]{1,0:T(1,128)} custom-call(f32[128,128]{1,0:T(8,128)S(1)} %bitcast.7, s32[1,512]{1,0:T(1,128)S(1)} %get-tuple-element.20.target_ref), custom_call_target="tpu_custom_call" | custom-call | tf_op jit(solution)/shard_map/unpack/pallas_call | solution.py:281
  (2 shorter events, 0.0 us)
Async XLA Ops:
  56.1 3.7 %collective-permute-start = (bf16[512,896]{1,0:T(8,128)(2,1)S(1)}, bf16[512,896]{1,0:T(8,128)(2,1)S(1)}, u32[]{:S(2)}, u32[]{:S(2)}) collective-permute-start(bf16[512,896]{1,0:T(8,128)(2,1)S(1)} %hand.1.given_ref), channel_id=1, source_target_pairs={{0,4},{4,0},{1,5},{5,1},{2,6},{6,2},{3,7},{7,3},{8,12},{12,8},{9,1... | collective-permute-start | bytes 2752520 | tf_op jit(solution)/shard_map/swap/ppermute | solution.py:220
  60.7 1.4 %collective-permute-start.1 = (f32[128,128]{1,0:T(8,128)S(1)}, f32[128,128]{1,0:T(8,128)S(1)}, u32[]{:S(2)}, u32[]{:S(2)}) collective-permute-start(f32[128,128]{1,0:T(8,128)S(1)} %get-tuple-element.19), channel_id=1, source_target_pairs={{0,4},{4,0},{1,5},{5,1},{2,6},{6,2},{3,7},{7,3},{8,12},{12,8},{9,1... | collective-permute-start | bytes 196616 | tf_op jit(solution)/shard_map/ppermute | solution.py:220

commit v7 on v6

--- a/solution.py
+++ b/solution.py
@@ -100,15 +100,13 @@
     out_ref[:, :, CAP * width :] = ranks.astype(jnp.bfloat16).reshape(CHIPS, 2, LANES)
 
 
-def hand(rows_ref, out_ref):
-    chips, _, wide = rows_ref.shape
-    pairs = 2 * chips
+def hand(rows_ref, *out_refs):
+    _, _, wide = rows_ref.shape
     width = (wide - LANES) // CAP
-    for u in range(2):
-        place = slice(u * pairs, (u + 1) * pairs)
+    for u, ref in enumerate(out_refs):
         start = (2 + u) * width
-        out_ref[place, :width] = rows_ref[:, :, start : start + width].reshape(pairs, width)
-        out_ref[place, width:] = rows_ref[:, :, CAP * width :].reshape(pairs, LANES)
+        ref[:, :width] = rows_ref[:, :, start : start + width].reshape(TILE, width)
+        ref[:, width:] = rows_ref[:, :, CAP * width :].reshape(TILE, LANES)
 
 
 def weights(dims, dim, b):
@@ -162,7 +160,7 @@
     return out
 
 
-def score_here(rows_ref, given_ref, keys_ref, down_ref, begun_ref, out_ref, best_ref):
+def score_here(rows_ref, first_ref, second_ref, keys_ref, down_ref, begun_ref, out_ref, best_ref):
     _, _, wide = rows_ref.shape
     _, width = keys_ref.shape
     digits = rows_ref[:, :, CAP * width :].reshape(TILE, LANES)
@@ -171,7 +169,7 @@
         place = slice(u * TILE, (u + 1) * TILE)
         keys_ref[place, :] = rows_ref[:, :, u * width : (u + 1) * width].reshape(TILE, width)
         down_ref[place, :] = down[u]
-    keys = blocks_of(keys_ref) + [given_ref[u * TILE : (u + 1) * TILE, :width] for u in range(2)]
+    keys = blocks_of(keys_ref) + [ref[:, :width] for ref in (first_ref, second_ref)]
     best = [jnp.full((TILE, LANES), -1.0, jnp.float32)] * CAP
     raise_best(best, keys, down, across, [(0, 0), (0, 1), (1, 1)])
     for u in range(2):
@@ -180,16 +178,31 @@
     out_ref[...] = gather_best(best[2:], best_ref, CAP)
 
 
-def score_swapped(keys_ref, down_ref, begun_ref, here_ref, got_ref, digit_ref, mine_ref, theirs_ref, best_ref):
-    across = [None] * 2 + [ranks_of(digits, 2 + u)[1] for u, digits in enumerate(blocks_of(digit_ref))]
-    best = blocks_of(begun_ref) + [jnp.full((TILE, LANES), -1.0, jnp.float32)] * 2
-    pairs = [(0, 2), (1, 2), (0, 3), (1, 3)]
-    raise_best(best, blocks_of(keys_ref) + blocks_of(got_ref), blocks_of(down_ref), across, pairs)
-    mine = jnp.maximum(gather_best(best[:2], best_ref.at[0], 0), here_ref[...])
-    for ref, found in ((mine_ref, mine), (theirs_ref, gather_best(best[2:], best_ref.at[1], CAP))):
-        ref[...] = found
-        ref[0:1, :] = found[LEAD : LEAD + 1, :]
-        ref[LEAD : LEAD + 1, :] = found[0:1, :]
+def score_first(keys_ref, down_ref, begun_ref, got_ref, digit_ref, raised_ref):
+    across = [None] * 2 + [ranks_of(digit_ref[...], 2)[1]]
+    best = blocks_of(begun_ref) + [jnp.full((TILE, LANES), -1.0, jnp.float32)]
+    raise_best(best, blocks_of(keys_ref) + [got_ref[...]], blocks_of(down_ref), across, [(0, 2), (1, 2)])
+    for u in range(3):
+        raised_ref[u * TILE : (u + 1) * TILE, :] = best[u]
+
+
+def put(ref, found):
+    ref[...] = found
+    ref[0:1, :] = found[LEAD : LEAD + 1, :]
+    ref[LEAD : LEAD + 1, :] = found[0:1, :]
+
+
+def score_second(keys_ref, down_ref, raised_ref, got_ref, digit_ref, final_ref, theirs_ref, best_ref):
+    across = [None] * 2 + [ranks_of(digit_ref[...], 3)[1]]
+    best = blocks_of(raised_ref) + [jnp.full((TILE, LANES), -1.0, jnp.float32)]
+    raise_best(best, blocks_of(keys_ref) + [got_ref[...]], blocks_of(down_ref), across, [(0, 2), (1, 2)])
+    put(theirs_ref, gather_best([raised_ref[2 * TILE :, :], best[2]], best_ref, CAP))
+    for u in range(2):
+        final_ref[u * TILE : (u + 1) * TILE, :] = best[u]
+
+
+def settle(final_ref, here_ref, mine_ref, best_ref):
+    put(mine_ref, jnp.maximum(gather_best(blocks_of(final_ref), best_ref, 0), here_ref[...]))
 
 
 def unpack(back_ref, target_ref, out_ref):
@@ -242,17 +255,16 @@
         name="pack",
     )(*map(off_chip, (cluster_ids.reshape(1, rows), ranks.reshape(1, rows), embeddings)))
     arrived = on_chip(exchange(packed, OUT_GROUPS))
+    half = slots // 2
     given = pl.pallas_call(
         hand,
-        out_shape=pltpu.VMEM((slots // 2, width + LANES), bf16),
+        out_shape=(pltpu.VMEM((TILE, width + LANES), bf16),) * 2,
         in_specs=[VMEM],
-        out_specs=VMEM,
+        out_specs=(VMEM,) * 2,
         compiler_params=LIMIT,
         name="hand",
     )(arrived)
-    with jax.named_scope("swap"):
-        got = swap(given)
-    half = slots // 2
+    got = [swap(part) for part in given]
     keys, down, begun, here = pl.pallas_call(
         score_here,
         out_shape=(
@@ -261,21 +273,38 @@
             pltpu.VMEM((half, LANES), f32),
             pltpu.VMEM((CHIPS, LANES), f32),
         ),
-        in_specs=[VMEM] * 2,
+        in_specs=[VMEM] * 3,
         out_specs=(VMEM,) * 4,
         scratch_shapes=[pltpu.VMEM((half, LANES), f32)],
         compiler_params=LIMIT,
         name="score_here",
-    )(arrived, on_chip(given))
-    mine, theirs = pl.pallas_call(
-        score_swapped,
-        out_shape=(pltpu.VMEM((CHIPS, LANES), f32),) * 2,
-        in_specs=[VMEM] * 6,
+    )(arrived, *map(on_chip, given))
+    raised = pl.pallas_call(
+        score_first,
+        out_shape=pltpu.VMEM((3 * TILE, LANES), f32),
+        in_specs=[VMEM] * 5,
+        out_specs=VMEM,
+        compiler_params=LIMIT,
+        name="score_first",
+    )(*map(on_chip, (keys, down, begun, got[0][:, :width], got[0][:, width:])))
+    final, theirs = pl.pallas_call(
+        score_second,
+        out_shape=(pltpu.VMEM((half, LANES), f32), pltpu.VMEM((CHIPS, LANES), f32)),
+        in_specs=[VMEM] * 5,
         out_specs=(VMEM, VMEM),
-        scratch_shapes=[pltpu.VMEM((2, half, LANES), f32)],
-        compiler_params=LIMIT,
-        name="score_swapped",
-    )(*map(on_chip, (keys, down, begun, here, got[:, :width], got[:, width:])))
+        scratch_shapes=[pltpu.VMEM((half, LANES), f32)],
+        compiler_params=LIMIT,
+        name="score_second",
+    )(*map(on_chip, (keys, down, raised, got[1][:, :width], got[1][:, width:])))
+    mine = pl.pallas_call(
+        settle,
+        out_shape=pltpu.VMEM((CHIPS, LANES), f32),
+        in_specs=[VMEM] * 2,
+        out_specs=VMEM,
+        scratch_shapes=[pltpu.VMEM((half, LANES), f32)],
+        compiler_params=LIMIT,
+        name="settle",
+    )(on_chip(final), on_chip(here))
     best = jnp.maximum(mine, swap(theirs))
     back = exchange(best.reshape(CHIPS, 1, LANES), BACK_GROUPS).reshape(CHIPS, LANES)
     out = pl.pallas_call(

time: 78.3 us -> 78 us (level)
    ppermute x2 -> x3, waiting for transfers between devices: 1.88 us -> 1.13 us  [swap(): return lax.ppermute(x, AXES, PARTNER)]
    ppermute x2 -> x3, starting transfers between devices: 2.1 us -> 2.2 us  [swap(): return lax.ppermute(x, AXES, PARTNER)]
  transfers between devices with their start and end apart: 2 -> 3, of which waited for: 2 -> 3; matrix products, arithmetic and copies ran while one was open for 0% -> 0% of each run, Pallas kernels for 1% -> 2%
where the time goes in v7:
time: 78 us; the launch traced here: 77.7 us
  blocking collectives  68.3 us (88%)
  Pallas kernels  5.93 us (8%)
  starting transfers between devices  2.2 us (3%)
  waiting for transfers between devices  1.13 us (1%)
    all_to_all x2, blocking collectives, exchange(): return lax.all_to_all(x, AXES, 0, 0, axis_index_groups=groups, tiled=True)  68.3 us
    pallas_call x1, Pallas kernels, shards(): pl.pallas_call(pack, out_shape=(pltpu.VMEM((CHIPS, 2, wide), bf16), pltpu...  2.61 us
    ppermute x3, starting transfers between devices, swap(): return lax.ppermute(x, AXES, PARTNER)  2.2 us
  transfers between devices with their start and end apart: 3, of which 3 were waited for; matrix products, arithmetic and copies ran while one was open for 0% of the time, Pallas kernels for 2%

profile of v7, /device:TPU:1, one launch (start us, length us, event | category | flops | bytes accessed | tf_op | source)
XLA Modules:
  0.0 77.7 jit_solution(1906287160474567211)
XLA Ops:
  0.0 2.6 %pack.1 = (bf16[128,2,3200]{2,1,0:T(2,128)(2,1)S(1)}, s32[1,512]{1,0:T(1,128)S(1)}) custom-call(s32[1,512]{1,0:T(1,128)} %bitcast.9, s32[1,512]{1,0:T(1,128)} %bitcast.10, bf16[512,768]{1,0:T(8,128)(2,1)} %rows_hbm.1), custom_call_target="tpu_custom_call" | custom-call | tf_op jit(solution)/shard_map/pack/pallas_call | solution.py:241
  2.6 53.3 %all_to_all.10.rows_ref = bf16[128,2,3200]{2,1,0:T(2,128)(2,1)S(1)} all-to-all(bf16[128,2,3200]{2,1,0:T(2,128)(2,1)S(1)} %get-tuple-element.15), channel_id=1, replica_groups={{179,0,1,2,3,8,9,10,11,16,17,18,19,24,25,26,27,32,33,34,35,40,41,42,43,..., dimensions={0} | all-to-all | bytes 3276800 | tf_op jit(solution)/shard_map/all_to_all | solution.py:229
  55.9 0.2 hand.1
  56.1 1.6 %collective-permute-start = (bf16[256,896]{1,0:T(8,128)(2,1)S(1)}, bf16[256,896]{1,0:T(8,128)(2,1)S(1)}, u32[]{:S(2)}, u32[]{:S(2)}) collective-permute-start(bf16[256,896]{1,0:T(8,128)(2,1)S(1)} %get-tuple-element.16.first_ref), channel_id=1, source_target_pairs={{0,4},{4,0},{1,5},{5,1},{2,6},{6,2},{3,7},{7,3},{8,12},{12,8},{9,1... | collective-permute-start | bytes 1376264 | tf_op jit(solution)/shard_map/ppermute | solution.py:233
  57.7 0.1 collective-permute-start.1
  57.8 1.1 %score_here.1 = (bf16[512,768]{1,0:T(8,128)(2,1)S(1)}, f32[512,128]{1,0:T(8,128)S(1)}, f32[512,128]{1,0:T(8,128)S(1)}, f32[128,128]{1,0:T(8,128)S(1)}) custom-call(bf16[128,2,3200]{2,1,0:T(2,128)(2,1)S(1)} %all_to_all.10.rows_ref, bf16[256,896]{1,0:T(8,128)(2,1)S(1)} %get-tuple-element.16.first_ref, bf16[256,896]{1,0:T(8,128)(2,1)S(1)} %get-tuple-element.17.second_ref), custom_call_target="tpu_custom_call" | custom-call | tf_op jit(solution)/shard_map/score_here/pallas_call | solution.py:268
  59.0 0.2 collective-permute-done
  59.2 0.4 score_first.1.raised_ref
  59.7 0.2 collective-permute-done.1
  59.9 0.6 score_second.1
  60.4 0.5 collective-permute-start.2
  60.9 0.2 settle.1
  61.1 0.7 collective-permute-done.2
  61.8 15.0 %all_to_all.11 = f32[128,1,128]{2,1,0:T(1,128)S(1)} all-to-all(f32[128,1,128]{2,1,0:T(1,128)S(1)} %bitcast.8), channel_id=1, replica_groups={{146,0,1,2,3,8,9,10,11,16,17,18,19,24,25,26,27,32,33,34,35,40,41,42,43,..., dimensions={0} | all-to-all | bytes 131072 | tf_op jit(solution)/shard_map/all_to_all | solution.py:229
  76.8 0.9 %unpack.1 = f32[1,512]{1,0:T(1,128)} custom-call(f32[128,128]{1,0:T(8,128)S(1)} %bitcast.7, s32[1,512]{1,0:T(1,128)S(1)} %get-tuple-element.24.target_ref), custom_call_target="tpu_custom_call" | custom-call | tf_op jit(solution)/shard_map/unpack/pallas_call | solution.py:310
  (5 shorter events, 0.1 us)
Async XLA Ops:
  56.1 3.1 %collective-permute-start = (bf16[256,896]{1,0:T(8,128)(2,1)S(1)}, bf16[256,896]{1,0:T(8,128)(2,1)S(1)}, u32[]{:S(2)}, u32[]{:S(2)}) collective-permute-start(bf16[256,896]{1,0:T(8,128)(2,1)S(1)} %get-tuple-element.16.first_ref), channel_id=1, source_target_pairs={{0,4},{4,0},{1,5},{5,1},{2,6},{6,2},{3,7},{7,3},{8,12},{12,8},{9,1... | collective-permute-start | bytes 1376264 | tf_op jit(solution)/shard_map/ppermute | solution.py:233
  57.7 2.1 %collective-permute-start.1 = (bf16[256,896]{1,0:T(8,128)(2,1)S(1)}, bf16[256,896]{1,0:T(8,128)(2,1)S(1)}, u32[]{:S(2)}, u32[]{:S(2)}) collective-permute-start(bf16[256,896]{1,0:T(8,128)(2,1)S(1)} %get-tuple-element.17.second_ref), channel_id=1, source_target_pairs={{0,4},{4,0},{1,5},{5,1},{2,6},{6,2},{3,7},{7,3},{8,12},{12,8},{9,1... | collective-permute-start | bytes 1376264 | tf_op jit(solution)/shard_map/ppermute | solution.py:233
  60.4 1.4 %collective-permute-start.2 = (f32[128,128]{1,0:T(8,128)S(1)}, f32[128,128]{1,0:T(8,128)S(1)}, u32[]{:S(2)}, u32[]{:S(2)}) collective-permute-start(f32[128,128]{1,0:T(8,128)S(1)} %get-tuple-element.23), channel_id=1, source_target_pairs={{0,4},{4,0},{1,5},{5,1},{2,6},{6,2},{3,7},{7,3},{8,12},{12,8},{9,1... | collective-permute-start | bytes 196616 | tf_op jit(solution)/shard_map/ppermute | solution.py:233
